TPU v7x, 256 devices: a whole 4x4x8 slice. The times are simulated.
256 devices in a mesh: gz: 16 (over z, y_lo), gy: 16 (over x, y_hi, core).
Axes of the slice: x: 4, y: 4 (y_hi: 2, y_lo: 2; y = y_hi * 2 + y_lo), z: 8, core: 2. Of those that a mesh axis runs over, the one named last changes fastest.
Arguments:
- charge: float32 [3145728], P(('gz', 'gy')), may hold values from -4 to 4
- fractions: float32 [3, 3145728], P(None, ('gz', 'gy')), may hold values from 0 to 1
- cell_base: int32 [3, 3145728], P(None, ('gz', 'gy')), may hold values from 0 to 255, as said below
- live_blocks: int32 [16, 16], P('gz'), may hold values from 12 to 96, as said below
- send_blocks: int32 [16, 16], P('gz'), may hold values from 0 to 36, as said below
- moduli: float32 [3, 256], replicated, may hold values from 0.5 to 2
- screening: float32 [1], replicated, may hold values from 8 to 16
Outputs:
- forces: float32 [3, 3145728], P(None, ('gz', 'gy'))
Inputs may be any that keep to these rules, and one draw needn't show every extreme that they name: `cell_base`: row 0 lies in 0 to 15, row 1 in 0 to 15, row 2 in 0 to 255. `live_blocks`: a domain's live blocks are its first ones; in every row of the table some domain has 96 live blocks. send_blocks is at most the domain's live blocks; live_blocks minus send_blocks plus send_blocks of the domain before it along gy (cyclically) is at most 96; in every row some domain sends 36.
All inputs are finite; a program needn't handle non-finite values.
Results may differ from a plain program's by a relative error of at most 0.00023.
Values sent between devices are 32-bit elements; how exact they have to be, the bound alone decides.
A program may use at most 64 MiB of HBM per device.

v0:
```python
import functools

import jax
import jax.numpy as jnp
import numpy as np
from jax import lax
from jax.experimental import pallas as pl
from jax.experimental.pallas import tpu as pltpu
from jax.sharding import PartitionSpec as P

GRID = 256
BLOCK = 128
ATOMS_DEV = 12288
SEND_MAX = 36
NPEER = 16
CHUNK = 512
ROWS = 384
MSG_Z = 40
MSG_Y = 32
MESH = pl.DeviceIdType.MESH
BF16 = jnp.bfloat16
F32 = jnp.float32


def split_np(table):
    table = np.asarray(table, np.float32)
    high = table.astype(jnp.bfloat16)
    low = (table - high.astype(np.float32)).astype(jnp.bfloat16)
    return high, low


def kz_of(block, local):
    j = 8 * block + local // 2
    return np.where(local % 2 == 0, j, np.where(j == 0, 128, (256 - j) % 256))


def forward_x():
    x = np.arange(256)[:, None]
    k = np.arange(128)[None, :]
    angle = 2 * np.pi * ((x * k) % 256) / 256
    table = np.concatenate([np.cos(angle), -np.sin(angle)], 1)
    table[:, 128] = (-1.0) ** np.arange(256)
    return table


def inverse_x():
    k = np.arange(128)[:, None]
    x = np.arange(256)[None, :]
    angle = 2 * np.pi * ((x * k) % 256) / 256
    table = np.concatenate([2 * np.cos(angle), -2 * np.sin(angle)], 0) / 256
    table[0] = 1.0 / 256
    table[128] = (-1.0) ** np.arange(256) / 256
    return table


def message_rows_z():
    part = np.zeros(MSG_Z, np.int64)
    place = np.zeros(MSG_Z, np.int64)
    for c in range(2):
        part[16 * c : 16 * c + 16] = c
        place[16 * c : 16 * c + 16] = np.arange(16)
        part[32 + 4 * c : 36 + 4 * c] = c
        place[32 + 4 * c : 36 + 4 * c] = 16 + np.arange(4)
    return part, place


def complex_table(part_out, wave, part_in, place):
    angle = 2 * np.pi * ((wave[:, None] * place[None, :]) % 256) / 256
    cosine, sine = np.cos(angle), np.sin(angle)
    same = part_out[:, None] == part_in[None, :]
    sign = np.where(part_out[:, None] == 0, 1.0, -1.0)
    return np.where(same, cosine, sign * sine)


def forward_z():
    local, part, block = np.meshgrid(np.arange(16), np.arange(2), np.arange(16), indexing="ij")
    wave = kz_of(block, local).reshape(-1)
    part = part.reshape(-1)
    part_in, place = message_rows_z()
    place_all = (16 * np.arange(16)[:, None] + place[None, :]).reshape(-1)
    table = complex_table(part, wave, np.tile(part_in, 16), place_all)
    pad = np.tile(place == 19, 16)
    return np.where(pad[None, :], 0.0, table)


def forward_y():
    part, wave = np.meshgrid(np.arange(2), np.arange(256), indexing="ij")
    block, part_in, place = np.meshgrid(np.arange(16), np.arange(2), np.arange(16), indexing="ij")
    return complex_table(
        part.reshape(-1), wave.reshape(-1), part_in.reshape(-1), (16 * block + place).reshape(-1)
    )


def split(value):
    high = value.astype(BF16)
    low = (value - high.astype(F32)).astype(BF16)
    return high, low


def spline_weights(t):
    remain = 1.0 - t
    square = t * t
    cubed = square * t
    sixth = 1.0 / 6.0
    weights = [
        remain * remain * remain * sixth,
        (3.0 * cubed - 6.0 * square + 4.0) * sixth,
        (-3.0 * cubed + 3.0 * square + 3.0 * t + 1.0) * sixth,
        cubed * sixth,
    ]
    return weights


def spline_slopes(t):
    remain = 1.0 - t
    square = t * t
    return [
        -0.5 * remain * remain,
        1.5 * square - 2.0 * t,
        -1.5 * square + t + 0.5,
        0.5 * square,
    ]


def wide(row, count):
    return jnp.broadcast_to(row, (count, row.shape[1]))


def stencil(rows, offset, cell, weights):
    place = offset - wide(cell, rows)
    table = jnp.zeros((rows, cell.shape[1]), F32)
    for k in range(3, -1, -1):
        table = jnp.where(place == k, wide(weights[k], rows), table)
    return table


def narrow_tables(cells, weights, row):
    n = cells.shape[1]
    cell = cells[row : row + 1]
    picked = [w[row : row + 1] for w in weights]
    iota = lax.broadcasted_iota(jnp.int32, (16, n), 0)
    main = stencil(16, iota, cell, picked)
    halo = stencil(8, 16 + (iota[:8] & 3), cell, picked)
    return main, halo


def x_table(hi_refs_pairs, cells, n):
    cell = cells[2:3]
    keys = [wide(((cell + m) & 255).astype(F32), 16).astype(BF16) for m in range(4)]
    sets = []
    for ref, weights in hi_refs_pairs:
        sets.append((ref, [wide(w, 16).astype(BF16) for w in weights]))
    base = lax.broadcasted_iota(jnp.int32, (16, n), 0).astype(F32)
    zero = jnp.zeros((16, n), BF16)
    for tile in range(16):
        place = (base + float(16 * tile)).astype(BF16)
        hits = [place == key for key in keys]
        for ref, weights in sets:
            table = zero
            for m in range(3, -1, -1):
                table = jnp.where(hits[m], weights[m], table)
            ref[16 * tile : 16 * tile + 16, :] = table


def nt_dot(a, b):
    return lax.dot_general(a, b, (((1,), (1,)), ((), ())), preferred_element_type=F32)


def nn_dot(a, b):
    return lax.dot_general(a, b, (((1,), (0,)), ((), ())), preferred_element_type=F32)


def tn_dot(a, b):
    return lax.dot_general(a, b, (((0,), (0,)), ((), ())), preferred_element_type=F32)


def pair_pattern(table, pair):
    n = table.shape[1]
    iota = lax.broadcasted_iota(jnp.int32, (8, n), 0)
    return jnp.where(
        iota < 4, wide(table[2 * pair : 2 * pair + 1], 8), wide(table[2 * pair + 1 : 2 * pair + 2], 8)
    )


def spread_kernel(live_ref, charge_ref, frac_ref, cell_ref, out_ref, a_hi, a_lo, x_hi, x_lo):
    n = CHUNK
    me = lax.axis_index("gy")
    live = live_ref[0, me] * BLOCK

    def build(first, slot):
        q = charge_ref[:, pl.ds(first, n)]
        lanes = first + lax.broadcasted_iota(jnp.int32, (1, n), 1)
        q = jnp.where(lanes < live, q, 0.0)
        t = frac_ref[:, pl.ds(first, n)]
        cells = cell_ref[:, pl.ds(first, n)]
        weights = spline_weights(t)
        along = [w[2:3] * q for w in weights]
        high = [w.astype(BF16).astype(F32) for w in along]
        low = [w - h for w, h in zip(along, high)]
        x_table([(x_hi.at[slot], high), (x_lo.at[slot], low)], cells, n)
        z_main, z_halo = narrow_tables(cells, weights, 0)
        y_main, y_halo = narrow_tables(cells, weights, 1)

        def put(row, value):
            upper, lower = split(value)
            a_hi[slot, row : row + 16, :] = upper
            a_lo[slot, row : row + 16, :] = lower

        for y in range(16):
            put(16 * y, wide(y_main[y : y + 1], 16) * z_main)
        for y in range(3):
            put(320 + 16 * y, wide(y_halo[y : y + 1], 16) * z_main)
        for quad in range(4):
            put(
                256 + 16 * quad,
                jnp.concatenate(
                    [pair_pattern(y_main, 2 * quad + h) * z_halo for h in range(2)], 0
                ),
            )
        put(368, jnp.concatenate([pair_pattern(y_halo, h) * z_halo for h in range(2)], 0))

    def multiply(slot):
        out_ref[...] += (
            nt_dot(a_hi[slot], x_hi[slot])
            + nt_dot(a_hi[slot], x_lo[slot])
            + nt_dot(a_lo[slot], x_hi[slot])
        )

    out_ref[...] = jnp.zeros_like(out_ref)
    build(0, 0)

    def step(i, carry):
        build(pl.multiple_of((2 * i + 1) * n, n), 1)
        multiply(0)
        build(pl.multiple_of(lax.min(2 * i + 2, 2 * pairs - 2) * n, n), 0)
        multiply(1)
        return carry

    pairs = ATOMS_DEV // (2 * n)
    lax.fori_loop(0, pairs, step, 0)


def spread(live_blocks, charge, fractions, cells):
    return pl.pallas_call(
        spread_kernel,
        out_shape=jax.ShapeDtypeStruct((ROWS, GRID), F32),
        in_specs=[pl.BlockSpec(memory_space=pltpu.SMEM)]
        + [pl.BlockSpec(memory_space=pltpu.VMEM)] * 3,
        out_specs=pl.BlockSpec(memory_space=pltpu.VMEM),
        scratch_shapes=[
            pltpu.VMEM((2, ROWS, CHUNK), BF16),
            pltpu.VMEM((2, ROWS, CHUNK), BF16),
            pltpu.VMEM((2, GRID, CHUNK), BF16),
            pltpu.VMEM((2, GRID, CHUNK), BF16),
        ],
        name="spread",
    )(live_blocks, charge, fractions, cells)


def gather_kernel(
    live_ref, pot_ref, charge_ref, frac_ref, cell_ref, out_ref, p_hi, p_lo, w_hi, w_lo, s_hi, s_lo
):
    n = CHUNK
    me = lax.axis_index("gy")
    live = live_ref[0, me] * BLOCK
    upper, lower = split(pot_ref[...])
    p_hi[...] = upper
    p_lo[...] = lower

    def build(first, slot):
        t = frac_ref[:, pl.ds(first, n)]
        cells = cell_ref[:, pl.ds(first, n)]
        sets = []
        for values, hi_ref, lo_ref in (
            ([w[2:3] for w in spline_weights(t)], w_hi, w_lo),
            ([w[2:3] for w in spline_slopes(t)], s_hi, s_lo),
        ):
            high = [w.astype(BF16).astype(F32) for w in values]
            low = [w - h for w, h in zip(values, high)]
            sets += [(hi_ref.at[slot], high), (lo_ref.at[slot], low)]
        x_table(sets, cells, n)

    def consume(first, slot):
        q = charge_ref[:, pl.ds(first, n)]
        lanes = first + lax.broadcasted_iota(jnp.int32, (1, n), 1)
        q = jnp.where(lanes < live, q, 0.0)
        t = frac_ref[:, pl.ds(first, n)]
        cells = cell_ref[:, pl.ds(first, n)]
        weights = spline_weights(t)
        slopes = spline_slopes(t)
        zw_main, zw_halo = narrow_tables(cells, weights, 0)
        zs_main, zs_halo = narrow_tables(cells, slopes, 0)
        yw_main, yw_halo = narrow_tables(cells, weights, 1)
        ys_main, ys_halo = narrow_tables(cells, slopes, 1)
        hi, lo = p_hi[...], p_lo[...]
        along = nn_dot(hi, w_hi[slot]) + nn_dot(hi, w_lo[slot]) + nn_dot(lo, w_hi[slot])
        steep = nn_dot(hi, s_hi[slot]) + nn_dot(hi, s_lo[slot]) + nn_dot(lo, s_hi[slot])
        zero = jnp.zeros((16, n), F32)
        sums = [zero, zero, zero]
        for y in range(19):
            row = 16 * y if y < 16 else 320 + 16 * (y - 16)
            yw = wide(yw_main[y : y + 1] if y < 16 else yw_halo[y - 16 : y - 15], 16)
            ys = wide(ys_main[y : y + 1] if y < 16 else ys_halo[y - 16 : y - 15], 16)
            piece, slope = along[row : row + 16], steep[row : row + 16]
            sums = [sums[0] + yw * piece, sums[1] + ys * piece, sums[2] + yw * slope]
        zero = jnp.zeros((8, n), F32)
        rims = [zero, zero, zero]
        for pair in range(10):
            row = 256 + 8 * pair if pair < 8 else 368 + 8 * (pair - 8)
            yw = pair_pattern(yw_main, pair) if pair < 8 else pair_pattern(yw_halo, pair - 8)
            ys = pair_pattern(ys_main, pair) if pair < 8 else pair_pattern(ys_halo, pair - 8)
            piece, slope = along[row : row + 8], steep[row : row + 8]
            rims = [rims[0] + yw * piece, rims[1] + ys * piece, rims[2] + yw * slope]
        force_z = sums[0] * zs_main
        force_y = sums[1] * zw_main
        force_x = sums[2] * zw_main
        force_z = force_z[:8] + force_z[8:] + rims[0] * zs_halo
        force_y = force_y[:8] + force_y[8:] + rims[1] * zw_halo
        force_x = force_x[:8] + force_x[8:] + rims[2] * zw_halo
        result = [jnp.sum(f, axis=0, keepdims=True) * -q for f in (force_z, force_y, force_x)]
        out_ref[:, pl.ds(first, n)] = jnp.concatenate(result, 0)

    build(0, 0)
    pairs = ATOMS_DEV // (2 * n)

    def step(i, carry):
        first = pl.multiple_of(2 * i * n, n)
        second = pl.multiple_of((2 * i + 1) * n, n)
        build(second, 1)
        consume(first, 0)
        build(pl.multiple_of(lax.min(2 * i + 2, 2 * pairs - 2) * n, n), 0)
        consume(second, 1)
        return carry

    lax.fori_loop(0, pairs, step, 0)


def gather(live_blocks, potential, charge, fractions, cells):
    return pl.pallas_call(
        gather_kernel,
        out_shape=jax.ShapeDtypeStruct((3, ATOMS_DEV), F32),
        in_specs=[pl.BlockSpec(memory_space=pltpu.SMEM)]
        + [pl.BlockSpec(memory_space=pltpu.VMEM)] * 4,
        out_specs=pl.BlockSpec(memory_space=pltpu.VMEM),
        scratch_shapes=[
            pltpu.VMEM((ROWS, GRID), BF16),
            pltpu.VMEM((ROWS, GRID), BF16),
        ]
        + [pltpu.VMEM((2, GRID, CHUNK), BF16)] * 4,
        name="gather",
    )(live_blocks, potential, charge, fractions, cells)


def turn(arrays):
    arrays = list(arrays)
    rows = arrays[0].shape[0]
    group = lax.broadcasted_iota(jnp.int32, (rows, 128), 1) >> 3
    for bit in range(4):
        g = 1 << bit
        keep = (group & g) == 0
        fresh = list(arrays)
        for i in range(16):
            if i & g == 0:
                low, high = arrays[i], arrays[i | g]
                fresh[i] = jnp.where(keep, low, pltpu.roll(high, 8 * g, 1))
                fresh[i | g] = jnp.where(keep, pltpu.roll(low, 128 - 8 * g, 1), high)
        arrays = fresh
    return arrays


def tables_of_influence(moduli_ref, screening, a, b):
    m = [moduli_ref[c : c + 1, :] for c in range(3)]
    lane_k = lax.broadcasted_iota(jnp.int32, (256, 256), 1)
    row_k = lax.broadcasted_iota(jnp.int32, (256, 256), 0)
    same = lane_k == row_k
    other = lane_k == ((256 - row_k) & 255)

    def column(row, mask):
        return jnp.sum(jnp.where(mask, wide(row, 256), 0.0), axis=1, keepdims=True)

    m0, m1, m2 = column(m[0], same), column(m[1], same), column(m[2], same)
    m1_back = column(m[1], other)

    lane = lax.broadcasted_iota(jnp.int32, (1, 128), 1)
    local, j = lane >> 3, lane & 7
    step = 8 * b + (local >> 1)
    kz = jnp.where(local & 1 == 0, step, jnp.where(step == 0, 128, 256 - step))
    kx = 8 * a + j
    rows = lax.broadcasted_iota(jnp.int32, (256, 128), 0)

    def along_lanes(col, index):
        hit = rows == wide(index, 256)
        return jnp.sum(jnp.where(hit, jnp.broadcast_to(col, (256, 128)), 0.0), 0, keepdims=True)

    z0, z1 = along_lanes(m0, kz), along_lanes(m0, (256 - kz) & 255)
    x0, x1 = along_lanes(m2, kx), along_lanes(m2, (256 - kx) & 255)
    xn = along_lanes(m2, jnp.full_like(kx, 128))

    def signed(k):
        return jnp.where(k < 128, k, k - 256)

    nz, ny = signed(kz), signed(rows)
    flat = ny * ny + wide(nz * nz, 256)

    def kernel_at(nx, first, second):
        radius = flat + wide(nx * nx, 256)
        squared = radius.astype(F32) / float(GRID * GRID)
        safe = jnp.where(radius > 0, squared, 1.0)
        product = m1 * wide(z0 * first, 256) + m1_back * wide(z1 * second, 256)
        return jnp.where(radius > 0, product * jnp.exp(-screening * squared) / safe, 0.0)

    at_kx = kernel_at(kx, x0, x1)
    at_last = kernel_at(jnp.full_like(kx, 128), xn, xn)
    packed = (rows >= 0) & wide(kx == 0, 256)
    straight = jnp.where(packed, 0.5 * (at_kx + at_last), at_kx)
    crossed = jnp.where(packed, 0.5 * (at_kx - at_last), 0.0)
    return straight, crossed


def solve_kernel(
    screening_ref,
    tile_ref,
    moduli_ref,
    fx_hi,
    fx_lo,
    gx_hi,
    gx_lo,
    fz_hi,
    fz_lo,
    fy_hi,
    fy_lo,
    out_ref,
    rim_in,
    send_1,
    recv_1,
    send_2,
    recv_2,
    send_3,
    recv_3,
    send_4,
    recv_4,
    straight_ref,
    crossed_ref,
    work,
    rim_sems,
    send_sems,
    recv_sems,
):
    a, b = lax.axis_index("gz"), lax.axis_index("gy")
    barrier = pltpu.get_barrier_semaphore()

    def greet(s, carry):
        pl.semaphore_signal(
            barrier, inc=1, device_id=((a + s) & 15, b), device_id_type=MESH
        )
        pl.semaphore_signal(
            barrier, inc=1, device_id=(a, (b + s) & 15), device_id_type=MESH
        )
        return carry

    lax.fori_loop(1, NPEER, greet, 0)
    pl.semaphore_wait(barrier, 2 * (NPEER - 1))

    def exchange(stage, src, dst, size, over_z):
        me = a if over_z else b

        def copy(peer, slot):
            return pltpu.make_async_remote_copy(
                src_ref=src.at[pl.ds(pl.multiple_of(peer * size, size), size), :],
                dst_ref=dst.at[pl.ds(pl.multiple_of(slot * size, size), size), :],
                send_sem=send_sems.at[stage, peer],
                recv_sem=recv_sems.at[stage, slot],
                device_id=(peer, b) if over_z else (a, peer),
                device_id_type=MESH,
            )

        def start(s, carry):
            copy((me + s) & 15, me).start()
            return carry

        def arrive(s, carry):
            peer = (me + s) & 15
            copy(peer, peer).wait_recv()
            return carry

        def leave(s, carry):
            copy((me + s) & 15, me).wait_send()
            return carry

        lax.fori_loop(1, NPEER, start, 0)
        own = pl.ds(pl.multiple_of(me * size, size), size)
        dst[own, :] = src[own, :]
        return (
            lambda: lax.fori_loop(1, NPEER, arrive, 0),
            lambda: lax.fori_loop(1, NPEER, leave, 0),
        )

    rim = pltpu.make_async_remote_copy(
        src_ref=tile_ref.at[pl.ds(320, 64), :],
        dst_ref=rim_in,
        send_sem=rim_sems.at[0],
        recv_sem=rim_sems.at[1],
        device_id=(a, (b + 1) & 15),
        device_id_type=MESH,
    )
    rim.start()
    straight, crossed = tables_of_influence(moduli_ref, screening_ref[0], a, b)
    straight_ref[...] = straight
    crossed_ref[...] = crossed
    rim.wait()
    work[...] = tile_ref[:320, :]
    work[0:48, :] += rim_in[0:48, :]
    work[256:272, :] += rim_in[48:64, :]

    high, low = split(work[...])
    spectrum = nn_dot(high, fx_hi[...]) + nn_dot(high, fx_lo[...]) + nn_dot(low, fx_hi[...])
    iota = lax.broadcasted_iota(jnp.int32, (8, 128), 0)
    pieces = []
    for y in range(16):
        real = spectrum[16 * y : 16 * y + 16, :128]
        imag = spectrum[16 * y : 16 * y + 16, 128:]
        row = 256 + 8 * (y // 2)
        rim_real, rim_imag = spectrum[row : row + 8, :128], spectrum[row : row + 8, 128:]
        if y % 2 == 0:
            halo = jnp.where(iota < 4, rim_real, pltpu.roll(rim_imag, 4, 0))
        else:
            halo = jnp.where(iota < 4, pltpu.roll(rim_real, 4, 0), rim_imag)
        pieces.append(jnp.concatenate([real, imag, halo], 0))
    for peer, piece in enumerate(turn(pieces)):
        send_1[MSG_Z * peer : MSG_Z * peer + MSG_Z, :] = piece
    arrive, leave_1 = exchange(0, send_1, recv_1, MSG_Z, True)
    arrive()

    high, low = split(recv_1[...])
    both = nn_dot(fz_hi[...], jnp.concatenate([high, low], 1))
    waves = both[:, :128] + both[:, 128:] + nn_dot(fz_lo[...], high)
    turned = turn([waves[32 * k : 32 * k + 32] for k in range(16)])
    for y in range(16):
        for c in range(2):
            send_2[pl.ds(16 * c + y, 16, stride=32), :] = turned[y][16 * c : 16 * c + 16]
    arrive, leave_2 = exchange(1, send_2, recv_2, MSG_Y, False)
    arrive()

    lines = recv_2[...]
    lane = lax.broadcasted_iota(jnp.int32, (512, 128), 1)
    row = lax.broadcasted_iota(jnp.int32, (512, 128), 0)
    odd = (lane >> 3) & 1
    swapped = jnp.where(odd == 0, pltpu.roll(lines, 120, 1), pltpu.roll(lines, 8, 1))
    swapped = jnp.where((lane < 16 * (b == 0).astype(jnp.int32)), lines, swapped)
    swapped = jnp.where((row >> 4) & 1 == 0, swapped, -swapped)
    high, low = split(jnp.concatenate([lines, swapped], 1))
    waves = nn_dot(fy_hi[...], high) + nn_dot(fy_hi[...], low) + nn_dot(fy_lo[...], high)
    straight = jnp.concatenate([straight_ref[...]] * 2, 0)
    crossed = jnp.concatenate([crossed_ref[...]] * 2, 0)
    high, low = split(waves[:, :128] * straight + waves[:, 128:] * crossed)
    both = tn_dot(fy_hi[...], jnp.concatenate([high, low], 1))
    send_3[...] = (both[:, :128] + both[:, 128:] + tn_dot(fy_lo[...], high)) * (1.0 / 256)
    arrive, leave_3 = exchange(2, send_3, recv_3, MSG_Y, False)
    arrive()

    pieces = []
    for y in range(16):
        pieces.append(
            jnp.concatenate(
                [recv_3[pl.ds(16 * c + y, 16, stride=32), :] for c in range(2)], 0
            )
        )
    high, low = split(jnp.concatenate(turn(pieces), 0))
    both = tn_dot(fz_hi[...], jnp.concatenate([high, low], 1))
    send_4[...] = (both[:, :128] + both[:, 128:] + tn_dot(fz_lo[...], high)) * (1.0 / 256)
    arrive, leave_4 = exchange(3, send_4, recv_4, MSG_Z, True)
    arrive()

    turned = turn([recv_4[MSG_Z * k : MSG_Z * k + MSG_Z, :] for k in range(16)])
    lines = [jnp.concatenate([t[0:16], t[16:32]], 1) for t in turned]
    for pair in range(8):
        even, odd = turned[2 * pair][32:40], turned[2 * pair + 1][32:40]
        real = jnp.where(iota < 4, even, pltpu.roll(odd, 4, 0))
        imag = jnp.where(iota < 4, pltpu.roll(even, 4, 0), odd)
        lines.append(jnp.concatenate([real, imag], 1))
    high, low = split(jnp.concatenate(lines, 0))
    out_ref[0:320, :] = (
        nn_dot(high, gx_hi[...]) + nn_dot(high, gx_lo[...]) + nn_dot(low, gx_hi[...])
    )

    rims = [
        pltpu.make_async_remote_copy(
            src_ref=out_ref.at[pl.ds(source, size), :],
            dst_ref=out_ref.at[pl.ds(target, size), :],
            send_sem=rim_sems.at[2 + 2 * k],
            recv_sem=rim_sems.at[3 + 2 * k],
            device_id=(a, (b + 15) & 15),
            device_id_type=MESH,
        )
        for k, (source, target, size) in enumerate(((0, 320, 48), (256, 368, 16)))
    ]
    for copy in rims:
        copy.start()
    leave_1()
    leave_2()
    leave_3()
    leave_4()
    for copy in rims:
        copy.wait()


def solve(tile, moduli, screening):
    tables = []
    for table in (forward_x(), inverse_x(), forward_z(), forward_y()):
        tables += [jnp.asarray(part) for part in split_np(table)]
    message_z = pltpu.VMEM((NPEER * MSG_Z, 128), F32)
    message_y = pltpu.VMEM((NPEER * MSG_Y, 128), F32)
    return pl.pallas_call(
        solve_kernel,
        out_shape=jax.ShapeDtypeStruct((ROWS, GRID), F32),
        in_specs=[pl.BlockSpec(memory_space=pltpu.SMEM)]
        + [pl.BlockSpec(memory_space=pltpu.VMEM)] * (2 + len(tables)),
        out_specs=pl.BlockSpec(memory_space=pltpu.VMEM),
        scratch_shapes=[pltpu.VMEM((64, GRID), F32)]
        + [message_z] * 2
        + [message_y] * 4
        + [message_z] * 2
        + [pltpu.VMEM((256, 128), F32)] * 2
        + [
            pltpu.VMEM((320, GRID), F32),
            pltpu.SemaphoreType.DMA((6,)),
            pltpu.SemaphoreType.DMA((4, NPEER)),
            pltpu.SemaphoreType.DMA((4, NPEER)),
        ],
        compiler_params=pltpu.CompilerParams(collective_id=0, has_side_effects=True),
        name="solve",
    )(screening, tile, moduli, *tables)


def body(charge, fractions, cell_base, live_blocks, send_blocks, moduli, screening):
    column = lax.axis_index("gy")
    before = (column + NPEER - 1) % NPEER
    lanes = lax.iota(jnp.int32, NPEER)

    def pick(table, index):
        return jnp.sum(jnp.where(lanes == index, table[0], 0))

    kept = (pick(live_blocks, column) - pick(send_blocks, column)) * BLOCK
    arriving = pick(send_blocks, before) * BLOCK

    charge = charge[None, :]
    tile = spread(live_blocks, charge, fractions, cell_base)
    potential = solve(tile, moduli, screening)
    home = gather(live_blocks, potential, charge, fractions, cell_base)

    margin = SEND_MAX * BLOCK
    padded = jnp.concatenate([home, jnp.zeros((3, margin), F32)], 1)
    lent = lax.dynamic_slice_in_dim(padded, kept, margin, 1)
    guests = lax.ppermute(lent, "gy", [(i, (i + 1) % NPEER) for i in range(NPEER)])
    places = lax.iota(jnp.int32, margin)
    guests = jnp.where(places < arriving, guests, 0.0)
    slots = lax.iota(jnp.int32, ATOMS_DEV + margin)
    own = jnp.where(slots < kept, padded, 0.0)
    return lax.dynamic_update_slice_in_dim(own, guests, kept, 1)[:, :ATOMS_DEV]


def solution(mesh):
    return jax.shard_map(
        body,
        mesh=mesh,
        in_specs=(
            P(("gz", "gy")),
            P(None, ("gz", "gy")),
            P(None, ("gz", "gy")),
            P("gz", None),
            P("gz", None),
            P(),
            P(),
        ),
        out_specs=P(None, ("gz", "gy")),
        check_vma=False,
    )
```

profile of v0, /device:TPU:8, one launch (start us, length us, event | category | flops | bytes accessed | tf_op | source)
XLA Modules:
  0.0 106.9 jit_solution(16793545927224765553)
XLA Ops:
  0.7 15.6 %spread.1.tile_ref = f32[384,256]{1,0:T(8,128)} custom-call(s32[1,16]{1,0:T(1,128)} %live_ref.3, f32[1,12288]{1,0:T(1,128)} %bitcast.6, f32[3,12288]{1,0:T(4,128)} %frac_ref.3, s32[3,12288]{1,0:T(4,128)} %cell_ref.3), custom_call_target="tpu_custom_call" | custom-call | tf_op jit(solution)/shard_map/spread/pallas_call | solution.py:244
  16.2 56.2 %solve.1.pot_ref = f32[384,256]{1,0:T(8,128)} custom-call(f32[1]{0:T(128)S(6)} %copy.17.screening_ref, f32[384,256]{1,0:T(8,128)} %spread.1.tile_ref, f32[3,256]{1,0:T(4,128)} %moduli_ref.1, bf16[256,256]{1,0:T(8,128)(2,1)} %constant.44.clone.fx_hi, bf16[256,256]{1,0:T(8,128)(2,1)} %constant.45.clone.fx_lo, bf16[256,256]{1,0:T(8,128)(2,1)} %constant.46.clone.gx_hi, ...), custom_call_target="tpu_custom_call" | custom-call | tf_op jit(solution)/shard_map/solve/pallas_call | solution.py:613
  72.4 0.0 copy-start.1
  72.4 0.0 copy-start.2
  72.4 23.4 %gather.1 = f32[3,12288]{1,0:T(4,128)} custom-call(s32[1,16]{1,0:T(1,128)} %live_ref.3, f32[384,256]{1,0:T(8,128)} %solve.1.pot_ref, f32[1,12288]{1,0:T(1,128)} %bitcast.7, f32[3,12288]{1,0:T(4,128)} %frac_ref.3, s32[3,12288]{1,0:T(4,128)} %cell_ref.3), custom_call_target="tpu_custom_call" | custom-call | tf_op jit(solution)/shard_map/gather/pallas_call | solution.py:339
  95.8 0.0 copy-start
  95.8 0.0 copy-done.1
  95.8 0.0 copy-done.2
  95.8 0.7 fusion.2
  97.8 0.9 pad_dynamic-slice_fusion
  98.7 0.7 collective-permute-start
  99.4 0.0 copy-done
  99.4 0.1 pad_select_fusion
  100.2 6.0 %collective-permute-done = f32[3,4608]{1,0:T(4,128)S(1)} collective-permute-done((f32[3,4608]{1,0:T(4,128)S(1)}, f32[3,4608]{1,0:T(4,128)S(1)}, u32[]{:S(2)}, u32[]{:S(2)}) %collective-permute-start) | collective-permute-done | bytes 55328 | tf_op jit(solution)/shard_map/ppermute | solution.py:654
  106.2 0.7 slice.4
  (3 shorter events, 0.1 us)
Async XLA Ops:
  72.4 23.5 %copy-start.1 = (s32[1,16]{1,0:T(1,128)S(1)}, s32[1,16]{1,0:T(1,128)}, u32[]{:S(2)}) copy-start(s32[1,16]{1,0:T(1,128)} %live_ref.3) | copy-start | bytes 196
  72.4 23.4 %copy-start.2 = (s32[1,16]{1,0:T(1,128)S(1)}, s32[1,16]{1,0:T(1,128)}, u32[]{:S(2)}) copy-start(s32[1,16]{1,0:T(1,128)} %param.19) | copy-start | bytes 196
  95.8 3.6 %copy-start = (f32[3,12288]{1,0:T(4,128)S(1)}, f32[3,12288]{1,0:T(4,128)}, u32[]{:S(2)}) copy-start(f32[3,12288]{1,0:T(4,128)} %gather.1) | copy-start | bytes 442372
  98.7 7.5 %collective-permute-start = (f32[3,4608]{1,0:T(4,128)S(1)}, f32[3,4608]{1,0:T(4,128)S(1)}, u32[]{:S(2)}, u32[]{:S(2)}) collective-permute-start(f32[3,4608]{1,0:T(4,128)S(1)} %pad_dynamic-slice_fusion), channel_id=1, source_target_pairs={{0,1},{1,2},{2,3},{3,4},{4,5},{5,6},{6,7},{7,8},{8,9},{9,10},{10,1... | collective-permute-start | bytes 165896 | tf_op jit(solution)/shard_map/ppermute | solution.py:654
where the time goes:
time: 107 us
  Pallas kernels  95.1 us (89%)
  waiting for transfers between devices  5.99 us (6%)
  between operations  2.61 us (2%)
  local copies, waits for them, and re-layouts  1.65 us (2%)
    pallas_call x1, Pallas kernels, solve(): pl.pallas_call(solve_kernel, out_shape=jax.ShapeDtypeStruct((ROWS, GRID),...  56.2 us
    pallas_call x1, Pallas kernels, gather(): pl.pallas_call(gather_kernel, out_shape=jax.ShapeDtypeStruct((3, ATOMS_DE...  23.4 us
    pallas_call x1, Pallas kernels, spread(): pl.pallas_call(spread_kernel, out_shape=jax.ShapeDtypeStruct((ROWS, GRID)...  15.6 us
    ppermute x1, waiting for transfers between devices, body(): lax.ppermute(lent, 'gy', [(i, (i + 1) % NPEER) for i in range(NPEER)])  5.99 us
  transfers between devices with their start and end apart: 1, of which 1 were waited for; matrix products, arithmetic and copies ran while one was open for 0% of the time, Pallas kernels for 0%

commit v1 on v0

v1 whole, which is shorter than its diff:
```python
import functools

import jax
import jax.numpy as jnp
import numpy as np
from jax import lax
from jax.experimental import pallas as pl
from jax.experimental.pallas import tpu as pltpu
from jax.sharding import PartitionSpec as P

GRID = 256
BLOCK = 128
ATOMS_DEV = 12288
NBLK = 96
SEND_MAX = 36
NPEER = 16
CHUNK = 512
SPREAD_UNROLL = 4
GATHER_UNROLL = 3
ROWS = 384
MSG_Z = 40
MSG_Y = 32
MESH = pl.DeviceIdType.MESH
BF16 = jnp.bfloat16
F32 = jnp.float32


def split_np(table):
    table = np.asarray(table, np.float32)
    high = table.astype(jnp.bfloat16)
    low = (table - high.astype(np.float32)).astype(jnp.bfloat16)
    return high, low


def kz_of(block, local):
    j = 8 * block + local // 2
    return np.where(local % 2 == 0, j, np.where(j == 0, 128, (256 - j) % 256))


def forward_x():
    x = np.arange(256)[:, None]
    k = np.arange(128)[None, :]
    angle = 2 * np.pi * ((x * k) % 256) / 256
    table = np.concatenate([np.cos(angle), -np.sin(angle)], 1)
    table[:, 128] = (-1.0) ** np.arange(256)
    return table


def inverse_x():
    k = np.arange(128)[:, None]
    x = np.arange(256)[None, :]
    angle = 2 * np.pi * ((x * k) % 256) / 256
    table = np.concatenate([2 * np.cos(angle), -2 * np.sin(angle)], 0) / 256
    table[0] = 1.0 / 256
    table[128] = (-1.0) ** np.arange(256) / 256
    return table


def message_rows_z():
    part = np.zeros(MSG_Z, np.int64)
    place = np.zeros(MSG_Z, np.int64)
    for c in range(2):
        part[16 * c : 16 * c + 16] = c
        place[16 * c : 16 * c + 16] = np.arange(16)
        part[32 + 4 * c : 36 + 4 * c] = c
        place[32 + 4 * c : 36 + 4 * c] = 16 + np.arange(4)
    return part, place


def complex_table(part_out, wave, part_in, place):
    angle = 2 * np.pi * ((wave[:, None] * place[None, :]) % 256) / 256
    cosine, sine = np.cos(angle), np.sin(angle)
    same = part_out[:, None] == part_in[None, :]
    sign = np.where(part_out[:, None] == 0, 1.0, -1.0)
    return np.where(same, cosine, sign * sine)


def forward_z():
    local, part, block = np.meshgrid(np.arange(16), np.arange(2), np.arange(16), indexing="ij")
    wave = kz_of(block, local).reshape(-1)
    part = part.reshape(-1)
    part_in, place = message_rows_z()
    place_all = (16 * np.arange(16)[:, None] + place[None, :]).reshape(-1)
    table = complex_table(part, wave, np.tile(part_in, 16), place_all)
    pad = np.tile(place == 19, 16)
    return np.where(pad[None, :], 0.0, table)


def forward_y():
    part, wave = np.meshgrid(np.arange(2), np.arange(256), indexing="ij")
    block, part_in, place = np.meshgrid(np.arange(16), np.arange(2), np.arange(16), indexing="ij")
    return complex_table(
        part.reshape(-1), wave.reshape(-1), part_in.reshape(-1), (16 * block + place).reshape(-1)
    )


def split(value):
    high = value.astype(BF16)
    low = (value - high.astype(F32)).astype(BF16)
    return high, low


def spline_weights(t):
    remain = 1.0 - t
    square = t * t
    cubed = square * t
    sixth = 1.0 / 6.0
    weights = [
        remain * remain * remain * sixth,
        (3.0 * cubed - 6.0 * square + 4.0) * sixth,
        (-3.0 * cubed + 3.0 * square + 3.0 * t + 1.0) * sixth,
        cubed * sixth,
    ]
    return weights


def spline_slopes(t):
    remain = 1.0 - t
    square = t * t
    return [
        -0.5 * remain * remain,
        1.5 * square - 2.0 * t,
        -1.5 * square + t + 0.5,
        0.5 * square,
    ]


def wide(row, count):
    return jnp.broadcast_to(row, (count, row.shape[1]))


def stencil(offset, cell, weights):
    rows = offset.shape[0]
    place = offset - wide(cell, rows)
    table = jnp.zeros(offset.shape, F32)
    for k in range(3, -1, -1):
        table = jnp.where(place == k, wide(weights[k], rows), table)
    return table


def narrow_tables(cells, weights, row):
    cell = cells[row : row + 1]
    picked = [w[row : row + 1] for w in weights]
    iota = lax.broadcasted_iota(jnp.int32, (16, cell.shape[1]), 0)
    return stencil(iota, cell, picked), stencil(16 + (iota[:8] & 3), cell, picked)


def x_tables(cells, weight_sets):
    cell = cells[2:3]
    keys = [wide(((cell + m) & 255).astype(F32), 16).astype(BF16) for m in range(4)]
    sets = [[wide(w, 16).astype(BF16) for w in weights] for weights in weight_sets]
    base = lax.broadcasted_iota(jnp.int32, (16, 128), 0).astype(F32)
    results = [[] for _ in sets]
    for tile in range(16):
        place = (base + float(16 * tile)).astype(BF16)
        tables = [jnp.zeros((16, 128), BF16) for _ in sets]
        for m in range(3, -1, -1):
            hit = place == keys[m]
            tables = [jnp.where(hit, weights[m], t) for weights, t in zip(sets, tables)]
        for result, table in zip(results, tables):
            result.append(table)
    return [jnp.concatenate(result, 0) for result in results]


def high_low(rows):
    high = [w.astype(BF16).astype(F32) for w in rows]
    return high, [w - h for w, h in zip(rows, high)]


def nt_dot(a, b):
    return lax.dot_general(a, b, (((1,), (1,)), ((), ())), preferred_element_type=F32)


def nn_dot(a, b):
    return lax.dot_general(a, b, (((1,), (0,)), ((), ())), preferred_element_type=F32)


def tn_dot(a, b):
    return lax.dot_general(a, b, (((0,), (0,)), ((), ())), preferred_element_type=F32)


def pair_pattern(table, pair):
    iota = lax.broadcasted_iota(jnp.int32, (8, table.shape[1]), 0)
    return jnp.where(
        iota < 4, wide(table[2 * pair : 2 * pair + 1], 8), wide(table[2 * pair + 1 : 2 * pair + 2], 8)
    )


def plane_tables(cells, weights):
    z_main, z_halo = narrow_tables(cells, weights, 0)
    y_main, y_halo = narrow_tables(cells, weights, 1)
    pieces = [wide(y_main[y : y + 1], 16) * z_main for y in range(16)]
    pieces += [pair_pattern(y_main, pair) * z_halo for pair in range(8)]
    pieces += [wide(y_halo[y : y + 1], 16) * z_main for y in range(3)]
    pieces += [pair_pattern(y_halo, pair) * z_halo for pair in range(2)]
    return split(jnp.concatenate(pieces, 0))


def spread_atoms(live, charge_ref, frac_ref, cell_ref, tile_ref):
    n = CHUNK
    tile_ref[...] = jnp.zeros_like(tile_ref)

    def chunk(first):
        q_all = charge_ref[:, pl.ds(first, n)]
        lanes = first + lax.broadcasted_iota(jnp.int32, (1, n), 1)
        q_all = jnp.where(lanes < live, q_all, 0.0)
        weights_all = spline_weights(frac_ref[:, pl.ds(first, n)])
        cells_all = cell_ref[:, pl.ds(first, n)]
        columns = []
        for group in range(n // 128):
            lanes = slice(128 * group, 128 * group + 128)
            weights = [w[:, lanes] for w in weights_all]
            cells, q = cells_all[:, lanes], q_all[:, lanes]
            columns.append(
                tuple(x_tables(cells, high_low([w[2:3] * q for w in weights])))
                + plane_tables(cells, weights)
            )
        x_hi, x_lo, a_hi, a_lo = (jnp.concatenate(part, 1) for part in zip(*columns))
        tile_ref[...] += nt_dot(a_hi, x_hi) + nt_dot(a_hi, x_lo) + nt_dot(a_lo, x_hi)

    def step(i, carry):
        for u in range(SPREAD_UNROLL):
            chunk(pl.multiple_of((SPREAD_UNROLL * i + u) * n, n))
        return carry

    lax.fori_loop(0, ATOMS_DEV // (n * SPREAD_UNROLL), step, 0)


def gather_atoms(chunks, charge_ref, frac_ref, cell_ref, out_ref, p_hi, p_lo):
    n = 256

    def piece_of(first):
        t = frac_ref[:, pl.ds(first, n)]
        cells_all = cell_ref[:, pl.ds(first, n)]
        weights_all, slopes_all = spline_weights(t), spline_slopes(t)
        columns = []
        for group in range(n // 128):
            lanes = slice(128 * group, 128 * group + 128)
            columns.append(
                x_tables(
                    cells_all[:, lanes],
                    high_low([w[2:3, lanes] for w in weights_all])
                    + high_low([w[2:3, lanes] for w in slopes_all]),
                )
            )
        w_hi, w_lo, s_hi, s_lo = (jnp.concatenate(part, 1) for part in zip(*columns))
        hi, lo = p_hi[...], p_lo[...]
        along_all = nn_dot(hi, w_hi) + nn_dot(hi, w_lo) + nn_dot(lo, w_hi)
        steep_all = nn_dot(hi, s_hi) + nn_dot(hi, s_lo) + nn_dot(lo, s_hi)
        results = []
        for group in range(n // 128):
            lanes = slice(128 * group, 128 * group + 128)
            along, steep = along_all[:, lanes], steep_all[:, lanes]
            weights = [w[:, lanes] for w in weights_all]
            slopes = [w[:, lanes] for w in slopes_all]
            cells = cells_all[:, lanes]
            zw_main, zw_halo = narrow_tables(cells, weights, 0)
            zs_main, zs_halo = narrow_tables(cells, slopes, 0)
            yw_main, yw_halo = narrow_tables(cells, weights, 1)
            ys_main, ys_halo = narrow_tables(cells, slopes, 1)
            sums = [jnp.zeros((16, 128), F32)] * 3
            for y in range(19):
                row = 16 * y if y < 16 else 320 + 16 * (y - 16)
                yw = wide(yw_main[y : y + 1] if y < 16 else yw_halo[y - 16 : y - 15], 16)
                ys = wide(ys_main[y : y + 1] if y < 16 else ys_halo[y - 16 : y - 15], 16)
                piece, slope = along[row : row + 16], steep[row : row + 16]
                sums = [sums[0] + yw * piece, sums[1] + ys * piece, sums[2] + yw * slope]
            rims = [jnp.zeros((8, 128), F32)] * 3
            for pair in range(10):
                row = 256 + 8 * pair if pair < 8 else 368 + 8 * (pair - 8)
                yw = pair_pattern(yw_main, pair) if pair < 8 else pair_pattern(yw_halo, pair - 8)
                ys = pair_pattern(ys_main, pair) if pair < 8 else pair_pattern(ys_halo, pair - 8)
                piece, slope = along[row : row + 8], steep[row : row + 8]
                rims = [rims[0] + yw * piece, rims[1] + ys * piece, rims[2] + yw * slope]
            sums = [sums[0] * zs_main, sums[1] * zw_main, sums[2] * zw_main]
            rims = [rims[0] * zs_halo, rims[1] * zw_halo, rims[2] * zw_halo]
            results.append(
                jnp.concatenate(
                    [
                        jnp.sum(f[:8] + f[8:] + r, axis=0, keepdims=True)
                        for f, r in zip(sums, rims)
                    ],
                    0,
                )
            )
        q = charge_ref[:, pl.ds(first, n)]
        out_ref[:, pl.ds(first, n)] = jnp.concatenate(results, 1) * -q

    low, high = chunks
    per_step = GATHER_UNROLL * CHUNK

    def step(i, carry):
        for u in range(per_step // n):
            piece_of(pl.multiple_of(low * CHUNK + i * per_step + u * n, n))
        return carry

    lax.fori_loop(0, (high - low) // GATHER_UNROLL, step, 0)


def turn(arrays):
    arrays = list(arrays)
    rows = arrays[0].shape[0]
    group = lax.broadcasted_iota(jnp.int32, (rows, 128), 1) >> 3
    for bit in range(4):
        g = 1 << bit
        keep = (group & g) == 0
        fresh = list(arrays)
        for i in range(16):
            if i & g == 0:
                low, high = arrays[i], arrays[i | g]
                fresh[i] = jnp.where(keep, low, pltpu.roll(high, 8 * g, 1))
                fresh[i | g] = jnp.where(keep, pltpu.roll(low, 128 - 8 * g, 1), high)
        arrays = fresh
    return arrays


def tables_of_influence(moduli_ref, screening, a, b):
    m = [moduli_ref[c : c + 1, :] for c in range(3)]
    lane_k = lax.broadcasted_iota(jnp.int32, (256, 256), 1)
    row_k = lax.broadcasted_iota(jnp.int32, (256, 256), 0)
    same = lane_k == row_k
    other = lane_k == ((256 - row_k) & 255)

    def column(row, mask):
        return jnp.sum(jnp.where(mask, wide(row, 256), 0.0), axis=1, keepdims=True)

    m0, m1, m2 = column(m[0], same), column(m[1], same), column(m[2], same)
    m1_back = column(m[1], other)

    lane = lax.broadcasted_iota(jnp.int32, (1, 128), 1)
    local, j = lane >> 3, lane & 7
    step = 8 * b + (local >> 1)
    kz = jnp.where(local & 1 == 0, step, jnp.where(step == 0, 128, 256 - step))
    kx = 8 * a + j
    rows = lax.broadcasted_iota(jnp.int32, (256, 128), 0)

    def along_lanes(col, index):
        hit = rows == wide(index, 256)
        return jnp.sum(jnp.where(hit, jnp.broadcast_to(col, (256, 128)), 0.0), 0, keepdims=True)

    z0, z1 = along_lanes(m0, kz), along_lanes(m0, (256 - kz) & 255)
    x0, x1 = along_lanes(m2, kx), along_lanes(m2, (256 - kx) & 255)
    xn = along_lanes(m2, jnp.full_like(kx, 128))

    def signed(k):
        return jnp.where(k < 128, k, k - 256)

    nz, ny = signed(kz), signed(rows)
    flat = ny * ny + wide(nz * nz, 256)

    def kernel_at(nx, first, second):
        radius = flat + wide(nx * nx, 256)
        squared = radius.astype(F32) / float(GRID * GRID)
        safe = jnp.where(radius > 0, squared, 1.0)
        product = m1 * wide(z0 * first, 256) + m1_back * wide(z1 * second, 256)
        return jnp.where(radius > 0, product * jnp.exp(-screening * squared) / safe, 0.0)

    at_kx = kernel_at(kx, x0, x1)
    at_last = kernel_at(jnp.full_like(kx, 128), xn, xn)
    packed = (rows >= 0) & wide(kx == 0, 256)
    straight = jnp.where(packed, 0.5 * (at_kx + at_last), at_kx)
    crossed = jnp.where(packed, 0.5 * (at_kx - at_last), 0.0)
    return straight, crossed


def block(ref, index):
    return ref[:, BLOCK * index : BLOCK * index + BLOCK]


def shift_left(blocks, amount, top, keep):
    bit = top
    while bit:
        take = wide((amount & bit) > 0, blocks[0].shape[0])
        count = min(len(blocks), keep + bit - 1)
        last = len(blocks) - 1
        blocks = [
            jnp.where(take, blocks[min(i + bit, last)], blocks[i]) for i in range(count)
        ]
        bit //= 2
    return blocks


def handed_first(live, kept, charge_ref, frac_ref, cell_ref, charge_out, frac_out, cell_out):
    home = NBLK - SEND_MAX
    start = jnp.minimum(jnp.full((1, BLOCK), kept, jnp.int32), home)
    count = jnp.full((1, BLOCK), live, jnp.int32)
    charges = [jnp.where(count > i, block(charge_ref, i), 0.0) for i in range(NBLK)]
    for blocks, out in (
        (charges, charge_out),
        ([block(frac_ref, i) for i in range(NBLK)], frac_out),
        ([block(cell_ref, i) for i in range(NBLK)], cell_out),
    ):
        ordered = shift_left(blocks, start, 32, SEND_MAX) + blocks[:home]
        for i, value in enumerate(ordered):
            out[:, BLOCK * i : BLOCK * i + BLOCK] = value


def place_forces(kept, kept_before, arriving, forces, guests, out_ref):
    home = NBLK - SEND_MAX
    kept = jnp.full((1, BLOCK), kept, jnp.int32)
    kept_before = jnp.full((1, BLOCK), kept_before, jnp.int32)
    end = kept + arriving
    skip = kept_before - jnp.minimum(kept_before, home)
    arrived = shift_left([block(guests, i) for i in range(SEND_MAX)], skip, 32, SEND_MAX)
    placed = arrived + [jnp.zeros((3, BLOCK), F32)] * (NBLK - SEND_MAX)
    bit = 64
    while bit:
        take = wide((kept & bit) > 0, 3)
        placed = [
            jnp.where(take, placed[i - bit] if i >= bit else 0.0, placed[i]) for i in range(NBLK)
        ]
        bit //= 2
    for slot in range(NBLK):
        own = block(forces, SEND_MAX + slot if slot < home else slot - home)
        guest = jnp.where(wide(end > slot, 3), placed[slot], 0.0)
        out_ref[:, BLOCK * slot : BLOCK * slot + BLOCK] = jnp.where(wide(kept > slot, 3), own, guest)


def offsets_z():
    return [(dz, dy) for dz in (4, 3, -3, 2, -2, 1, -1, 0) for dy in (1, 0) if (dz, dy) != (0, 0)]


def offsets_y():
    moves = [(dx, dy, dc) for dx in (2, 1, -1, 0) for dy in (1, 0) for dc in (1, 0)]
    moves.remove((0, 0, 0))
    return sorted(moves, key=lambda m: -(abs(m[0]) + 2 * m[1]))


def solve_kernel(
    live_ref,
    send_ref,
    screening_ref,
    charge_ref,
    frac_ref,
    cell_ref,
    moduli_ref,
    fx_hi,
    fx_lo,
    gx_hi,
    gx_lo,
    fz_hi,
    fz_lo,
    fy_hi,
    fy_lo,
    out_ref,
    tile_ref,
    pot_ref,
    rim_in,
    send_1,
    recv_1,
    send_2,
    recv_2,
    send_3,
    recv_3,
    send_4,
    recv_4,
    straight_ref,
    crossed_ref,
    work,
    p_hi,
    p_lo,
    forces,
    guests,
    charge_in_order,
    frac_in_order,
    cell_in_order,
    rim_sems,
    send_sems,
    recv_sems,
):
    a, b = lax.axis_index("gz"), lax.axis_index("gy")
    barrier = pltpu.get_barrier_semaphore()
    peers_z = [
        ((a // 2 + dz + 8) % 8) * 2 + (a + dy) % 2 for dz, dy in offsets_z()
    ]
    peers_y = [
        ((b // 4 + dx + 4) % 4) * 4 + ((b // 2 + dy) % 2) * 2 + (b + dc) % 2
        for dx, dy, dc in offsets_y()
    ]
    for peer in peers_z:
        pl.semaphore_signal(barrier, inc=1, device_id=(peer, b), device_id_type=MESH)
    for peer in peers_y:
        pl.semaphore_signal(barrier, inc=1, device_id=(a, peer), device_id_type=MESH)

    before = (b + 15) % 16
    live = live_ref[0, b]
    kept = live - send_ref[0, b]
    kept_before = live_ref[0, before] - send_ref[0, before]
    arriving = send_ref[0, before]
    spread_atoms(live * BLOCK, charge_ref, frac_ref, cell_ref, tile_ref)
    pl.semaphore_wait(barrier, 2 * (NPEER - 1))

    def exchange(stage, src, dst, size, over_z):
        me = a if over_z else b
        peers = peers_z if over_z else peers_y

        def copy(peer, slot):
            return pltpu.make_async_remote_copy(
                src_ref=src.at[pl.ds(pl.multiple_of(peer * size, 8), size), :],
                dst_ref=dst.at[pl.ds(pl.multiple_of(slot * size, 8), size), :],
                send_sem=send_sems.at[stage, peer],
                recv_sem=recv_sems.at[stage, slot],
                device_id=(peer, b) if over_z else (a, peer),
                device_id_type=MESH,
            )

        for peer in peers:
            copy(peer, me).start()
        own = pl.ds(pl.multiple_of(me * size, 8), size)
        dst[own, :] = src[own, :]

        def arrive():
            for peer in peers:
                copy(peer, peer).wait_recv()

        def leave():
            for peer in peers:
                copy(peer, me).wait_send()

        return arrive, leave

    rim = pltpu.make_async_remote_copy(
        src_ref=tile_ref.at[pl.ds(320, 64), :],
        dst_ref=rim_in,
        send_sem=rim_sems.at[0],
        recv_sem=rim_sems.at[1],
        device_id=(a, (b + 1) % 16),
        device_id_type=MESH,
    )
    rim.start()
    rim.wait()
    work[...] = tile_ref[:320, :]
    work[0:48, :] += rim_in[0:48, :]
    work[256:272, :] += rim_in[48:64, :]

    high, low = split(work[...])
    spectrum = nn_dot(high, fx_hi[...]) + nn_dot(high, fx_lo[...]) + nn_dot(low, fx_hi[...])
    iota = lax.broadcasted_iota(jnp.int32, (8, 128), 0)
    pieces = []
    for y in range(16):
        real = spectrum[16 * y : 16 * y + 16, :128]
        imag = spectrum[16 * y : 16 * y + 16, 128:]
        row = 256 + 8 * (y // 2)
        rim_real, rim_imag = spectrum[row : row + 8, :128], spectrum[row : row + 8, 128:]
        if y % 2 == 0:
            halo = jnp.where(iota < 4, rim_real, pltpu.roll(rim_imag, 4, 0))
        else:
            halo = jnp.where(iota < 4, pltpu.roll(rim_real, 4, 0), rim_imag)
        pieces.append(jnp.concatenate([real, imag, halo], 0))
    for peer, piece in enumerate(turn(pieces)):
        send_1[MSG_Z * peer : MSG_Z * peer + MSG_Z, :] = piece
    arrive, leave_1 = exchange(0, send_1, recv_1, MSG_Z, True)
    straight, crossed = tables_of_influence(moduli_ref, screening_ref[0], a, b)
    straight_ref[...] = straight
    crossed_ref[...] = crossed
    arrive()

    high, low = split(recv_1[...])
    both = nn_dot(fz_hi[...], jnp.concatenate([high, low], 1))
    waves = both[:, :128] + both[:, 128:] + nn_dot(fz_lo[...], high)
    turned = turn([waves[32 * k : 32 * k + 32] for k in range(16)])
    for y in range(16):
        for c in range(2):
            send_2[pl.ds(16 * c + y, 16, stride=32), :] = turned[y][16 * c : 16 * c + 16]
    arrive, leave_2 = exchange(1, send_2, recv_2, MSG_Y, False)
    handed_first(
        live, kept, charge_ref, frac_ref, cell_ref, charge_in_order, frac_in_order, cell_in_order
    )
    arrive()

    lines = recv_2[...]
    lane = lax.broadcasted_iota(jnp.int32, (512, 128), 1)
    row = lax.broadcasted_iota(jnp.int32, (512, 128), 0)
    odd = (lane >> 3) & 1
    swapped = jnp.where(odd == 0, pltpu.roll(lines, 120, 1), pltpu.roll(lines, 8, 1))
    swapped = jnp.where((lane < 16 * (b == 0).astype(jnp.int32)), lines, swapped)
    swapped = jnp.where((row >> 4) & 1 == 0, swapped, -swapped)
    high, low = split(jnp.concatenate([lines, swapped], 1))
    waves = nn_dot(fy_hi[...], high) + nn_dot(fy_hi[...], low) + nn_dot(fy_lo[...], high)
    straight = jnp.concatenate([straight_ref[...]] * 2, 0)
    crossed = jnp.concatenate([crossed_ref[...]] * 2, 0)
    high, low = split(waves[:, :128] * straight + waves[:, 128:] * crossed)
    both = tn_dot(fy_hi[...], jnp.concatenate([high, low], 1))
    send_3[...] = (both[:, :128] + both[:, 128:] + tn_dot(fy_lo[...], high)) * (1.0 / 256)
    arrive, leave_3 = exchange(2, send_3, recv_3, MSG_Y, False)
    arrive()

    pieces = []
    for y in range(16):
        pieces.append(
            jnp.concatenate(
                [recv_3[pl.ds(16 * c + y, 16, stride=32), :] for c in range(2)], 0
            )
        )
    high, low = split(jnp.concatenate(turn(pieces), 0))
    both = tn_dot(fz_hi[...], jnp.concatenate([high, low], 1))
    send_4[...] = (both[:, :128] + both[:, 128:] + tn_dot(fz_lo[...], high)) * (1.0 / 256)
    arrive, leave_4 = exchange(3, send_4, recv_4, MSG_Z, True)
    arrive()

    turned = turn([recv_4[MSG_Z * k : MSG_Z * k + MSG_Z, :] for k in range(16)])
    lines = [jnp.concatenate([t[0:16], t[16:32]], 1) for t in turned]
    for pair in range(8):
        even, odd = turned[2 * pair][32:40], turned[2 * pair + 1][32:40]
        real = jnp.where(iota < 4, even, pltpu.roll(odd, 4, 0))
        imag = jnp.where(iota < 4, pltpu.roll(even, 4, 0), odd)
        lines.append(jnp.concatenate([real, imag], 1))
    high, low = split(jnp.concatenate(lines, 0))
    pot_ref[0:320, :] = (
        nn_dot(high, gx_hi[...]) + nn_dot(high, gx_lo[...]) + nn_dot(low, gx_hi[...])
    )

    rims = [
        pltpu.make_async_remote_copy(
            src_ref=pot_ref.at[pl.ds(source, size), :],
            dst_ref=pot_ref.at[pl.ds(target, size), :],
            send_sem=rim_sems.at[2 + 2 * k],
            recv_sem=rim_sems.at[3 + 2 * k],
            device_id=(a, before),
            device_id_type=MESH,
        )
        for k, (source, target, size) in enumerate(((0, 320, 48), (256, 368, 16)))
    ]
    for copy in rims:
        copy.start()
    leave_1()
    leave_2()
    leave_3()
    leave_4()
    for copy in rims:
        copy.wait()
    high, low = split(pot_ref[...])
    p_hi[...] = high
    p_lo[...] = low

    lent_chunks = SEND_MAX * BLOCK // CHUNK

    def compute(low, high):
        gather_atoms(
            (low, high), charge_in_order, frac_in_order, cell_in_order, forces, p_hi, p_lo
        )

    compute(0, lent_chunks)
    hand_on = pltpu.make_async_remote_copy(
        src_ref=forces.at[:, pl.ds(0, SEND_MAX * BLOCK)],
        dst_ref=guests,
        send_sem=rim_sems.at[6],
        recv_sem=rim_sems.at[7],
        device_id=(a, (b + 1) % 16),
        device_id_type=MESH,
    )
    hand_on.start()
    compute(lent_chunks, ATOMS_DEV // CHUNK)
    hand_on.wait()
    place_forces(kept, kept_before, arriving, forces, guests, out_ref)


def solve(live_blocks, send_blocks, screening, charge, fractions, cells, moduli):
    tables = []
    for table in (forward_x(), inverse_x(), forward_z(), forward_y()):
        tables += [jnp.asarray(part) for part in split_np(table)]
    message_z = pltpu.VMEM((NPEER * MSG_Z, 128), F32)
    message_y = pltpu.VMEM((NPEER * MSG_Y, 128), F32)
    return pl.pallas_call(
        solve_kernel,
        out_shape=jax.ShapeDtypeStruct((3, ATOMS_DEV), F32),
        in_specs=[pl.BlockSpec(memory_space=pltpu.SMEM)] * 3
        + [pl.BlockSpec(memory_space=pltpu.VMEM)] * (4 + len(tables)),
        out_specs=pl.BlockSpec(memory_space=pltpu.VMEM),
        scratch_shapes=[pltpu.VMEM((ROWS, GRID), F32)] * 2
        + [pltpu.VMEM((64, GRID), F32)]
        + [message_z] * 2
        + [message_y] * 4
        + [message_z] * 2
        + [pltpu.VMEM((256, 128), F32)] * 2
        + [pltpu.VMEM((320, GRID), F32)]
        + [pltpu.VMEM((ROWS, GRID), BF16)] * 2
        + [
            pltpu.VMEM((3, ATOMS_DEV), F32),
            pltpu.VMEM((3, SEND_MAX * BLOCK), F32),
            pltpu.VMEM((1, ATOMS_DEV), F32),
            pltpu.VMEM((3, ATOMS_DEV), F32),
            pltpu.VMEM((3, ATOMS_DEV), jnp.int32),
            pltpu.SemaphoreType.DMA((8,)),
            pltpu.SemaphoreType.DMA((4, NPEER)),
            pltpu.SemaphoreType.DMA((4, NPEER)),
        ],
        compiler_params=pltpu.CompilerParams(collective_id=0, has_side_effects=True),
        name="forces",
    )(live_blocks, send_blocks, screening, charge, fractions, cells, moduli, *tables)


def body(charge, fractions, cell_base, live_blocks, send_blocks, moduli, screening):
    return solve(
        live_blocks, send_blocks, screening, charge[None, :], fractions, cell_base, moduli
    )


def solution(mesh):
    return jax.shard_map(
        body,
        mesh=mesh,
        in_specs=(
            P(("gz", "gy")),
            P(None, ("gz", "gy")),
            P(None, ("gz", "gy")),
            P("gz", None),
            P("gz", None),
            P(),
            P(),
        ),
        out_specs=P(None, ("gz", "gy")),
        check_vma=False,
    )
```

time: 107 us -> 84.2 us (0.79)
  the two profiles are of different devices: /device:TPU:8 before, /device:TPU:1 now
where the time goes in v1:
time: 84.2 us; the launch traced here: 84.1 us
  Pallas kernels  81.8 us (97%)
  local copies, waits for them, and re-layouts  1.64 us (2%)
    pallas_call x1, Pallas kernels, solve(): pl.pallas_call(solve_kernel, out_shape=jax.ShapeDtypeStruct((3, ATOMS_DEV...  81.8 us

profile of v1, /device:TPU:1, one launch (start us, length us, event | category | flops | bytes accessed | tf_op | source)
XLA Modules:
  0.0 84.1 jit_solution(2908572970489755596)
XLA Ops:
  0.7 81.8 %forces.1 = f32[3,12288]{1,0:T(4,128)} custom-call(s32[1,16]{1,0:T(1,128)} %live_ref.1, s32[1,16]{1,0:T(1,128)} %send_ref.1, f32[1]{0:T(128)S(6)} %copy.17.screening_ref, f32[1,12288]{1,0:T(1,128)} %bitcast.1, f32[3,12288]{1,0:T(4,128)} %frac_ref.1, s32[3,12288]{1,0:T(4,128)} %cell_ref.1, f32[3,256]{1,0:T(4,128)} %moduli_ref.1, ...), custom_call_target="tpu_custom_call" | custom-call | tf_op jit(solution)/shard_map/forces/pallas_call | solution.py:664
  82.4 1.6 %copy.18 = f32[3,12288]{1,0:T(4,128)} copy(f32[3,12288]{1,0:T(4,128)} %forces.1) | data formatting | bytes 294912

commit v2 on v1

--- a/solution.py
+++ b/solution.py
@@ -16,10 +16,9 @@
 NPEER = 16
 CHUNK = 512
 SPREAD_UNROLL = 4
-GATHER_UNROLL = 3
+GATHER_UNROLL = 6
 ROWS = 384
-MSG_Z = 40
-MSG_Y = 32
+SLOT_Z = 24
 MESH = pl.DeviceIdType.MESH
 BF16 = jnp.bfloat16
 F32 = jnp.float32
@@ -37,61 +36,49 @@
     return np.where(local % 2 == 0, j, np.where(j == 0, 128, (256 - j) % 256))
 
 
+def kx_order():
+    stream, block, j = np.meshgrid(np.arange(2), np.arange(16), np.arange(4), indexing="ij")
+    return (8 * block + 4 * stream + j).reshape(2, 64)
+
+
 def forward_x():
     x = np.arange(256)[:, None]
-    k = np.arange(128)[None, :]
-    angle = 2 * np.pi * ((x * k) % 256) / 256
-    table = np.concatenate([np.cos(angle), -np.sin(angle)], 1)
-    table[:, 128] = (-1.0) ** np.arange(256)
-    return table
+    columns = []
+    for kx in kx_order():
+        angle = 2 * np.pi * ((x * kx[None, :]) % 256) / 256
+        last = np.where(kx[None, :] == 0, (-1.0) ** x, -np.sin(angle))
+        columns += [np.cos(angle), last]
+    return np.concatenate(columns, 1)
 
 
 def inverse_x():
-    k = np.arange(128)[:, None]
     x = np.arange(256)[None, :]
-    angle = 2 * np.pi * ((x * k) % 256) / 256
-    table = np.concatenate([2 * np.cos(angle), -2 * np.sin(angle)], 0) / 256
-    table[0] = 1.0 / 256
-    table[128] = (-1.0) ** np.arange(256) / 256
-    return table
-
-
-def message_rows_z():
-    part = np.zeros(MSG_Z, np.int64)
-    place = np.zeros(MSG_Z, np.int64)
-    for c in range(2):
-        part[16 * c : 16 * c + 16] = c
-        place[16 * c : 16 * c + 16] = np.arange(16)
-        part[32 + 4 * c : 36 + 4 * c] = c
-        place[32 + 4 * c : 36 + 4 * c] = 16 + np.arange(4)
-    return part, place
-
-
-def complex_table(part_out, wave, part_in, place):
-    angle = 2 * np.pi * ((wave[:, None] * place[None, :]) % 256) / 256
-    cosine, sine = np.cos(angle), np.sin(angle)
-    same = part_out[:, None] == part_in[None, :]
-    sign = np.where(part_out[:, None] == 0, 1.0, -1.0)
-    return np.where(same, cosine, sign * sine)
-
-
-def forward_z():
-    local, part, block = np.meshgrid(np.arange(16), np.arange(2), np.arange(16), indexing="ij")
+    rows = []
+    for kx in kx_order():
+        angle = 2 * np.pi * ((x * kx[:, None]) % 256) / 256
+        first = np.where(kx[:, None] == 0, 1.0, 2 * np.cos(angle))
+        last = np.where(kx[:, None] == 0, (-1.0) ** x, -2 * np.sin(angle))
+        rows += [first, last]
+    return np.concatenate(rows, 0) / 256
+
+
+def cos_sin(first, second):
+    angle = 2 * np.pi * ((first[:, None] * second[None, :]) % 256) / 256
+    return np.cos(angle), np.sin(angle)
+
+
+def tables_z():
+    local, block = np.meshgrid(np.arange(16), np.arange(16), indexing="ij")
     wave = kz_of(block, local).reshape(-1)
-    part = part.reshape(-1)
-    part_in, place = message_rows_z()
-    place_all = (16 * np.arange(16)[:, None] + place[None, :]).reshape(-1)
-    table = complex_table(part, wave, np.tile(part_in, 16), place_all)
-    pad = np.tile(place == 19, 16)
-    return np.where(pad[None, :], 0.0, table)
-
-
-def forward_y():
-    part, wave = np.meshgrid(np.arange(2), np.arange(256), indexing="ij")
-    block, part_in, place = np.meshgrid(np.arange(16), np.arange(2), np.arange(16), indexing="ij")
-    return complex_table(
-        part.reshape(-1), wave.reshape(-1), part_in.reshape(-1), (16 * block + place).reshape(-1)
-    )
+    place = np.arange(SLOT_Z)
+    places = (16 * np.arange(16)[:, None] + place[None, :]).reshape(-1)
+    pad = np.tile(place >= 19, 16)[None, :]
+    parts = [np.where(pad, 0.0, part) for part in cos_sin(wave, places)]
+    return np.concatenate(parts, 0), np.concatenate([part.T for part in parts], 0)
+
+
+def table_y():
+    return np.concatenate(cos_sin(np.arange(256), np.arange(256)), 0)
 
 
 def split(value):
@@ -226,7 +213,7 @@
     lax.fori_loop(0, ATOMS_DEV // (n * SPREAD_UNROLL), step, 0)
 
 
-def gather_atoms(chunks, charge_ref, frac_ref, cell_ref, out_ref, p_hi, p_lo):
+def gather_atoms(charge_ref, frac_ref, cell_ref, out_ref, p_hi, p_lo, when_lent_done):
     n = 256
 
     def piece_of(first):
@@ -286,21 +273,21 @@
         q = charge_ref[:, pl.ds(first, n)]
         out_ref[:, pl.ds(first, n)] = jnp.concatenate(results, 1) * -q
 
-    low, high = chunks
     per_step = GATHER_UNROLL * CHUNK
 
     def step(i, carry):
         for u in range(per_step // n):
-            piece_of(pl.multiple_of(low * CHUNK + i * per_step + u * n, n))
+            piece_of(pl.multiple_of(i * per_step + u * n, n))
+        pl.when(i == SEND_MAX * BLOCK // per_step)(when_lent_done)
         return carry
 
-    lax.fori_loop(0, (high - low) // GATHER_UNROLL, step, 0)
+    lax.fori_loop(0, ATOMS_DEV // per_step, step, 0)
 
 
 def turn(arrays):
     arrays = list(arrays)
     rows = arrays[0].shape[0]
-    group = lax.broadcasted_iota(jnp.int32, (rows, 128), 1) >> 3
+    group = lax.broadcasted_iota(jnp.int32, (rows, 128), 1) >> 2
     for bit in range(4):
         g = 1 << bit
         keep = (group & g) == 0
@@ -308,13 +295,13 @@
         for i in range(16):
             if i & g == 0:
                 low, high = arrays[i], arrays[i | g]
-                fresh[i] = jnp.where(keep, low, pltpu.roll(high, 8 * g, 1))
-                fresh[i | g] = jnp.where(keep, pltpu.roll(low, 128 - 8 * g, 1), high)
+                fresh[i] = jnp.where(keep, low, pltpu.roll(high, 4 * g, 1))
+                fresh[i | g] = jnp.where(keep, pltpu.roll(low, 128 - 4 * g, 1), high)
         arrays = fresh
     return arrays
 
 
-def tables_of_influence(moduli_ref, screening, a, b):
+def tables_of_influence(moduli_ref, screening, a, b, outs):
     m = [moduli_ref[c : c + 1, :] for c in range(3)]
     lane_k = lax.broadcasted_iota(jnp.int32, (256, 256), 1)
     row_k = lax.broadcasted_iota(jnp.int32, (256, 256), 0)
@@ -328,10 +315,9 @@
     m1_back = column(m[1], other)
 
     lane = lax.broadcasted_iota(jnp.int32, (1, 128), 1)
-    local, j = lane >> 3, lane & 7
+    local, j = (lane >> 2) & 15, lane & 3
     step = 8 * b + (local >> 1)
     kz = jnp.where(local & 1 == 0, step, jnp.where(step == 0, 128, 256 - step))
-    kx = 8 * a + j
     rows = lax.broadcasted_iota(jnp.int32, (256, 128), 0)
 
     def along_lanes(col, index):
@@ -339,28 +325,28 @@
         return jnp.sum(jnp.where(hit, jnp.broadcast_to(col, (256, 128)), 0.0), 0, keepdims=True)
 
     z0, z1 = along_lanes(m0, kz), along_lanes(m0, (256 - kz) & 255)
-    x0, x1 = along_lanes(m2, kx), along_lanes(m2, (256 - kx) & 255)
-    xn = along_lanes(m2, jnp.full_like(kx, 128))
-
     def signed(k):
         return jnp.where(k < 128, k, k - 256)
 
     nz, ny = signed(kz), signed(rows)
     flat = ny * ny + wide(nz * nz, 256)
 
-    def kernel_at(nx, first, second):
+    def kernel_at(kx):
+        nx = signed(kx)
         radius = flat + wide(nx * nx, 256)
         squared = radius.astype(F32) / float(GRID * GRID)
         safe = jnp.where(radius > 0, squared, 1.0)
+        first, second = along_lanes(m2, kx), along_lanes(m2, (256 - kx) & 255)
         product = m1 * wide(z0 * first, 256) + m1_back * wide(z1 * second, 256)
-        return jnp.where(radius > 0, product * jnp.exp(-screening * squared) / safe, 0.0)
-
-    at_kx = kernel_at(kx, x0, x1)
-    at_last = kernel_at(jnp.full_like(kx, 128), xn, xn)
-    packed = (rows >= 0) & wide(kx == 0, 256)
-    straight = jnp.where(packed, 0.5 * (at_kx + at_last), at_kx)
-    crossed = jnp.where(packed, 0.5 * (at_kx - at_last), 0.0)
-    return straight, crossed
+        value = product * jnp.exp(-screening * squared) / safe
+        return jnp.where(radius > 0, value, 0.0) * (1.0 / float(GRID * GRID))
+
+    kx = 8 * a + j
+    at_first, at_last = kernel_at(kx), kernel_at(jnp.full_like(kx, 128))
+    packed = wide(kx, 256) == 0
+    outs[0][...] = jnp.where(packed, 0.5 * (at_first + at_last), at_first)
+    outs[1][...] = kernel_at(kx + 4)
+    outs[2][...] = jnp.where(packed, 0.5 * (at_first - at_last), 0.0)
 
 
 def block(ref, index):
@@ -434,29 +420,36 @@
     frac_ref,
     cell_ref,
     moduli_ref,
-    fx_hi,
-    fx_lo,
-    gx_hi,
-    gx_lo,
-    fz_hi,
-    fz_lo,
-    fy_hi,
-    fy_lo,
+    fx_far,
+    gx_far,
+    fz_far,
+    gz_far,
+    fy_far,
     out_ref,
+    fx,
+    gx,
+    fz,
+    gz,
+    fy,
+    table_sems,
     tile_ref,
     pot_ref,
     rim_in,
-    send_1,
-    recv_1,
+    send_10,
+    recv_10,
+    send_11,
+    recv_11,
     send_2,
     recv_2,
     send_3,
     recv_3,
-    send_4,
-    recv_4,
-    straight_ref,
-    crossed_ref,
-    work,
+    send_40,
+    recv_40,
+    send_41,
+    recv_41,
+    straight_0,
+    straight_1,
+    crossed_0,
     p_hi,
     p_lo,
     forces,
@@ -464,7 +457,10 @@
     charge_in_order,
     frac_in_order,
     cell_in_order,
+    held_1,
+    held_4,
     rim_sems,
+    relay_sems,
     send_sems,
     recv_sems,
 ):
@@ -482,42 +478,89 @@
     for peer in peers_y:
         pl.semaphore_signal(barrier, inc=1, device_id=(a, peer), device_id_type=MESH)
 
+    loads = [
+        pltpu.make_async_copy(far, near, table_sems.at[k])
+        for k, (far, near) in enumerate(
+            ((fx_far, fx), (fz_far, fz), (fy_far, fy), (gz_far, gz), (gx_far, gx))
+        )
+    ]
+    for load in loads:
+        load.start()
+
     before = (b + 15) % 16
     live = live_ref[0, b]
     kept = live - send_ref[0, b]
     kept_before = live_ref[0, before] - send_ref[0, before]
     arriving = send_ref[0, before]
     spread_atoms(live * BLOCK, charge_ref, frac_ref, cell_ref, tile_ref)
+    for load in loads:
+        load.wait()
     pl.semaphore_wait(barrier, 2 * (NPEER - 1))
 
-    def exchange(stage, src, dst, size, over_z):
+    leaving = []
+
+    def exchange(stage, src, dst, size, over_z, relay=None):
         me = a if over_z else b
         peers = peers_z if over_z else peers_y
-
-        def copy(peer, slot):
+        whole = pl.ds(0, (NPEER - 1) * size)
+
+        def rows_of(index):
+            return pl.ds(pl.multiple_of(index * size, 8), size)
+
+        def copy(source, target, peer, send_sem, recv_sem):
             return pltpu.make_async_remote_copy(
-                src_ref=src.at[pl.ds(pl.multiple_of(peer * size, 8), size), :],
-                dst_ref=dst.at[pl.ds(pl.multiple_of(slot * size, 8), size), :],
-                send_sem=send_sems.at[stage, peer],
-                recv_sem=recv_sems.at[stage, slot],
+                src_ref=source,
+                dst_ref=target,
+                send_sem=send_sem,
+                recv_sem=recv_sem,
                 device_id=(peer, b) if over_z else (a, peer),
                 device_id_type=MESH,
             )
 
+        send_sem, recv_sem = send_sems.at[stage], recv_sems.at[stage]
+        passing = []
+        if relay is not None:
+            buffer, sems = relay
+            step = (a // 2 + 6) % 8 * 2
+            origin = (a // 2 + 2) % 8 * 2 + a % 2
+            for k in range(2):
+                held = buffer.at[pl.ds(k * size, size), :]
+                copy(
+                    src.at[rows_of(peers[k]), :], held, step + a % 2, send_sem, relay_sems.at[sems]
+                ).start()
+                passing.append(
+                    copy(
+                        held,
+                        dst.at[rows_of(origin), :],
+                        step + (a + 1 - k) % 2,
+                        relay_sems.at[sems + 1],
+                        recv_sem,
+                    )
+                )
+            peers = peers[2:]
         for peer in peers:
-            copy(peer, me).start()
-        own = pl.ds(pl.multiple_of(me * size, 8), size)
-        dst[own, :] = src[own, :]
-
-        def arrive():
-            for peer in peers:
-                copy(peer, peer).wait_recv()
-
-        def leave():
-            for peer in peers:
-                copy(peer, me).wait_send()
-
-        return arrive, leave
+            copy(src.at[rows_of(peer), :], dst.at[rows_of(me), :], peer, send_sem, recv_sem).start()
+        dst[rows_of(me), :] = src[rows_of(me), :]
+        every = copy(src.at[whole, :], dst.at[whole, :], peers[0], send_sem, recv_sem)
+        leaving.append(every.wait_send)
+        if relay is not None:
+            both = pl.ds(0, 2 * size)
+            held = copy(
+                buffer.at[both, :],
+                buffer.at[both, :],
+                peers[0],
+                relay_sems.at[sems + 1],
+                relay_sems.at[sems],
+            )
+            leaving.append(held.wait_send)
+
+            def forward():
+                held.wait_recv()
+                for message in passing:
+                    message.start()
+
+            return every.wait_recv, forward
+        return every.wait_recv
 
     rim = pltpu.make_async_remote_copy(
         src_ref=tile_ref.at[pl.ds(320, 64), :],
@@ -528,89 +571,142 @@
         device_id_type=MESH,
     )
     rim.start()
+
+    def transform_x(value):
+        high, low = split(value)
+        return nn_dot(high, fx[0]) + nn_dot(high, fx[1]) + nn_dot(low, fx[0])
+
+    spectrum = transform_x(tile_ref[0:320, :])
     rim.wait()
-    work[...] = tile_ref[:320, :]
-    work[0:48, :] += rim_in[0:48, :]
-    work[256:272, :] += rim_in[48:64, :]
-
-    high, low = split(work[...])
-    spectrum = nn_dot(high, fx_hi[...]) + nn_dot(high, fx_lo[...]) + nn_dot(low, fx_hi[...])
+    extra = transform_x(rim_in[...])
+    spectrum = jnp.concatenate(
+        [
+            spectrum[0:48] + extra[0:48],
+            spectrum[48:256],
+            spectrum[256:272] + extra[48:64],
+            spectrum[272:320],
+        ],
+        0,
+    )
     iota = lax.broadcasted_iota(jnp.int32, (8, 128), 0)
     pieces = []
     for y in range(16):
-        real = spectrum[16 * y : 16 * y + 16, :128]
-        imag = spectrum[16 * y : 16 * y + 16, 128:]
         row = 256 + 8 * (y // 2)
-        rim_real, rim_imag = spectrum[row : row + 8, :128], spectrum[row : row + 8, 128:]
+        first, second = spectrum[row : row + 8, :128], spectrum[row : row + 8, 128:]
         if y % 2 == 0:
-            halo = jnp.where(iota < 4, rim_real, pltpu.roll(rim_imag, 4, 0))
+            halo = jnp.where(iota < 4, first, pltpu.roll(second, 4, 0))
         else:
-            halo = jnp.where(iota < 4, pltpu.roll(rim_real, 4, 0), rim_imag)
-        pieces.append(jnp.concatenate([real, imag, halo], 0))
+            halo = jnp.where(iota < 4, pltpu.roll(first, 4, 0), second)
+        pieces.append(jnp.concatenate([spectrum[16 * y : 16 * y + 16, :128], halo], 0))
     for peer, piece in enumerate(turn(pieces)):
-        send_1[MSG_Z * peer : MSG_Z * peer + MSG_Z, :] = piece
-    arrive, leave_1 = exchange(0, send_1, recv_1, MSG_Z, True)
-    straight, crossed = tables_of_influence(moduli_ref, screening_ref[0], a, b)
-    straight_ref[...] = straight
-    crossed_ref[...] = crossed
-    arrive()
-
-    high, low = split(recv_1[...])
-    both = nn_dot(fz_hi[...], jnp.concatenate([high, low], 1))
-    waves = both[:, :128] + both[:, 128:] + nn_dot(fz_lo[...], high)
-    turned = turn([waves[32 * k : 32 * k + 32] for k in range(16)])
-    for y in range(16):
-        for c in range(2):
-            send_2[pl.ds(16 * c + y, 16, stride=32), :] = turned[y][16 * c : 16 * c + 16]
-    arrive, leave_2 = exchange(1, send_2, recv_2, MSG_Y, False)
+        send_10[24 * peer : 24 * peer + 24, :] = piece
+    arrive_10 = exchange(0, send_10, recv_10, 24, True)
+    for peer, piece in enumerate(turn([spectrum[16 * y : 16 * y + 16, 128:] for y in range(16)])):
+        send_11[16 * peer : 16 * peer + 16, :] = piece
+    arrive_11, forward = exchange(1, send_11, recv_11, 16, True, (held_1, 0))
+    tables_of_influence(
+        moduli_ref, screening_ref[0], a, b, (straight_0, straight_1, crossed_0)
+    )
+    forward()
+
+    half = lax.broadcasted_iota(jnp.int32, (1, 128), 1) < 64
+    forward_sign = jnp.where(half, 1.0, -1.0)
+
+    def product(table, value):
+        high, low = split(value)
+        width = value.shape[1]
+        both = nn_dot(table[0], jnp.concatenate([high, low], 1))
+        return both[:, :width] + both[:, width:] + nn_dot(table[1], high)
+
+    def joined(both, sign):
+        rows = both.shape[0] // 2
+        return both[:rows] + wide(sign, rows) * pltpu.roll(both[rows:], 64, 1)
+
+    def stage_z(stream):
+        if stream == 0:
+            lines = recv_10[...]
+        else:
+            lines = []
+            for k in range(16):
+                lines += [
+                    recv_11[16 * k : 16 * k + 16, :],
+                    pltpu.roll(recv_10[24 * k + 16 : 24 * k + 24, :], 4, 0),
+                ]
+            lines = jnp.concatenate(lines, 0)
+        waves = joined(product(fz, lines), forward_sign)
+        turned = turn([waves[16 * k : 16 * k + 16] for k in range(16)])
+        for y in range(16):
+            send_2[pl.ds(256 * stream + y, 16, stride=16), :] = turned[y]
+        rows = pl.ds(256 * stream, 256)
+        return exchange(2 + stream, send_2.at[rows, :], recv_2.at[rows, :], 16, False)
+
+    def stage_y(stream):
+        lines = recv_2[256 * stream : 256 * stream + 256, :]
+        if stream == 0:
+            lane = lax.broadcasted_iota(jnp.int32, (256, 128), 1)
+            odd = (lane >> 2) & 1
+            swapped = jnp.where(odd == 0, pltpu.roll(lines, 124, 1), pltpu.roll(lines, 4, 1))
+            own_pair = wide(((lax.broadcasted_iota(jnp.int32, (1, 128), 1) & 63) >> 3) + b, 256) == 0
+            swapped = jnp.where(own_pair, lines, swapped)
+            both = product(fy, jnp.concatenate([lines, swapped * wide(forward_sign, 256)], 1))
+            waves = joined(both[:, :128], forward_sign) * straight_0[...]
+            waves = waves + joined(both[:, 128:], forward_sign) * crossed_0[...]
+        else:
+            waves = joined(product(fy, lines), forward_sign) * straight_1[...]
+        rows = pl.ds(256 * stream, 256)
+        send_3[rows, :] = joined(product(fy, waves), -forward_sign)
+        return exchange(4 + stream, send_3.at[rows, :], recv_3.at[rows, :], 16, False)
+
+    def stage_z_back(stream):
+        pieces = [recv_3[pl.ds(256 * stream + y, 16, stride=16), :] for y in range(16)]
+        lines = jnp.concatenate(turn(pieces), 0)
+        return joined(product(gz, lines), -forward_sign)
+
+    arrive_10()
+    arrive_20 = stage_z(0)
+    arrive_11()
+    arrive_21 = stage_z(1)
+    arrive_20()
+    arrive_30 = stage_y(0)
+    arrive_21()
+    arrive_31 = stage_y(1)
+    arrive_30()
+    back = stage_z_back(0)
+    for k in range(16):
+        send_40[16 * k : 16 * k + 16, :] = back[24 * k : 24 * k + 16]
+        send_41[24 * k + 16 : 24 * k + 24, :] = back[24 * k + 16 : 24 * k + 24]
+    arrive_40 = exchange(6, send_40, recv_40, 16, True)
+    arrive_31()
+    back = stage_z_back(1)
+    for k in range(16):
+        send_41[24 * k : 24 * k + 16, :] = back[24 * k : 24 * k + 16]
+        send_41[24 * k + 16 : 24 * k + 24, :] += pltpu.roll(back[24 * k + 16 : 24 * k + 24], 4, 0)
+    arrive_41, forward = exchange(7, send_41, recv_41, 24, True, (held_4, 2))
     handed_first(
         live, kept, charge_ref, frac_ref, cell_ref, charge_in_order, frac_in_order, cell_in_order
     )
-    arrive()
-
-    lines = recv_2[...]
-    lane = lax.broadcasted_iota(jnp.int32, (512, 128), 1)
-    row = lax.broadcasted_iota(jnp.int32, (512, 128), 0)
-    odd = (lane >> 3) & 1
-    swapped = jnp.where(odd == 0, pltpu.roll(lines, 120, 1), pltpu.roll(lines, 8, 1))
-    swapped = jnp.where((lane < 16 * (b == 0).astype(jnp.int32)), lines, swapped)
-    swapped = jnp.where((row >> 4) & 1 == 0, swapped, -swapped)
-    high, low = split(jnp.concatenate([lines, swapped], 1))
-    waves = nn_dot(fy_hi[...], high) + nn_dot(fy_hi[...], low) + nn_dot(fy_lo[...], high)
-    straight = jnp.concatenate([straight_ref[...]] * 2, 0)
-    crossed = jnp.concatenate([crossed_ref[...]] * 2, 0)
-    high, low = split(waves[:, :128] * straight + waves[:, 128:] * crossed)
-    both = tn_dot(fy_hi[...], jnp.concatenate([high, low], 1))
-    send_3[...] = (both[:, :128] + both[:, 128:] + tn_dot(fy_lo[...], high)) * (1.0 / 256)
-    arrive, leave_3 = exchange(2, send_3, recv_3, MSG_Y, False)
-    arrive()
-
-    pieces = []
-    for y in range(16):
-        pieces.append(
-            jnp.concatenate(
-                [recv_3[pl.ds(16 * c + y, 16, stride=32), :] for c in range(2)], 0
-            )
-        )
-    high, low = split(jnp.concatenate(turn(pieces), 0))
-    both = tn_dot(fz_hi[...], jnp.concatenate([high, low], 1))
-    send_4[...] = (both[:, :128] + both[:, 128:] + tn_dot(fz_lo[...], high)) * (1.0 / 256)
-    arrive, leave_4 = exchange(3, send_4, recv_4, MSG_Z, True)
-    arrive()
-
-    turned = turn([recv_4[MSG_Z * k : MSG_Z * k + MSG_Z, :] for k in range(16)])
-    lines = [jnp.concatenate([t[0:16], t[16:32]], 1) for t in turned]
+    forward()
+    arrive_40()
+    turned_0 = turn([recv_40[16 * k : 16 * k + 16, :] for k in range(16)])
+    arrive_41()
+    turned_1 = turn([recv_41[24 * k : 24 * k + 24, :] for k in range(16)])
+
+    lines = [jnp.concatenate([first, second[:16]], 1) for first, second in zip(turned_0, turned_1)]
+    rims = []
     for pair in range(8):
-        even, odd = turned[2 * pair][32:40], turned[2 * pair + 1][32:40]
-        real = jnp.where(iota < 4, even, pltpu.roll(odd, 4, 0))
-        imag = jnp.where(iota < 4, pltpu.roll(even, 4, 0), odd)
-        lines.append(jnp.concatenate([real, imag], 1))
-    high, low = split(jnp.concatenate(lines, 0))
-    pot_ref[0:320, :] = (
-        nn_dot(high, gx_hi[...]) + nn_dot(high, gx_lo[...]) + nn_dot(low, gx_hi[...])
-    )
-
-    rims = [
+        even, odd = turned_1[2 * pair][16:24], turned_1[2 * pair + 1][16:24]
+        first = jnp.where(iota < 4, even, pltpu.roll(odd, 4, 0))
+        second = jnp.where(iota < 4, pltpu.roll(even, 4, 0), odd)
+        rims.append(jnp.concatenate([first, second], 1))
+
+    def back_x(value):
+        high, low = split(value)
+        return nn_dot(high, gx[0]) + nn_dot(high, gx[1]) + nn_dot(low, gx[0])
+
+    value = back_x(jnp.concatenate(lines[:3] + rims[:2], 0))
+    pot_ref[0:48, :] = value[0:48]
+    pot_ref[256:272, :] = value[48:64]
+    copies = [
         pltpu.make_async_remote_copy(
             src_ref=pot_ref.at[pl.ds(source, size), :],
             dst_ref=pot_ref.at[pl.ds(target, size), :],
@@ -621,26 +717,19 @@
         )
         for k, (source, target, size) in enumerate(((0, 320, 48), (256, 368, 16)))
     ]
-    for copy in rims:
+    for copy in copies:
         copy.start()
-    leave_1()
-    leave_2()
-    leave_3()
-    leave_4()
-    for copy in rims:
+    value = back_x(jnp.concatenate(lines[3:] + rims[2:], 0))
+    pot_ref[48:256, :] = value[:208]
+    pot_ref[272:320, :] = value[208:]
+    for leave in leaving:
+        leave()
+    for copy in copies:
         copy.wait()
     high, low = split(pot_ref[...])
     p_hi[...] = high
     p_lo[...] = low
 
-    lent_chunks = SEND_MAX * BLOCK // CHUNK
-
-    def compute(low, high):
-        gather_atoms(
-            (low, high), charge_in_order, frac_in_order, cell_in_order, forces, p_hi, p_lo
-        )
-
-    compute(0, lent_chunks)
     hand_on = pltpu.make_async_remote_copy(
         src_ref=forces.at[:, pl.ds(0, SEND_MAX * BLOCK)],
         dst_ref=guests,
@@ -649,31 +738,36 @@
         device_id=(a, (b + 1) % 16),
         device_id_type=MESH,
     )
-    hand_on.start()
-    compute(lent_chunks, ATOMS_DEV // CHUNK)
+    gather_atoms(
+        charge_in_order, frac_in_order, cell_in_order, forces, p_hi, p_lo, hand_on.start
+    )
     hand_on.wait()
     place_forces(kept, kept_before, arriving, forces, guests, out_ref)
 
 
 def solve(live_blocks, send_blocks, screening, charge, fractions, cells, moduli):
     tables = []
-    for table in (forward_x(), inverse_x(), forward_z(), forward_y()):
-        tables += [jnp.asarray(part) for part in split_np(table)]
-    message_z = pltpu.VMEM((NPEER * MSG_Z, 128), F32)
-    message_y = pltpu.VMEM((NPEER * MSG_Y, 128), F32)
+    for table in (forward_x(), inverse_x(), *tables_z(), table_y()):
+        tables.append(jnp.asarray(np.stack(split_np(table))))
+    short, tall = pltpu.VMEM((256, 128), F32), pltpu.VMEM((384, 128), F32)
+    both = pltpu.VMEM((512, 128), F32)
     return pl.pallas_call(
         solve_kernel,
         out_shape=jax.ShapeDtypeStruct((3, ATOMS_DEV), F32),
         in_specs=[pl.BlockSpec(memory_space=pltpu.SMEM)] * 3
-        + [pl.BlockSpec(memory_space=pltpu.VMEM)] * (4 + len(tables)),
+        + [pl.BlockSpec(memory_space=pltpu.VMEM)] * 4
+        + [pl.BlockSpec(memory_space=pltpu.HBM)] * len(tables),
         out_specs=pl.BlockSpec(memory_space=pltpu.VMEM),
-        scratch_shapes=[pltpu.VMEM((ROWS, GRID), F32)] * 2
+        scratch_shapes=[pltpu.VMEM(table.shape, BF16) for table in tables]
+        + [pltpu.SemaphoreType.DMA((len(tables),))]
+        + [pltpu.VMEM((ROWS, GRID), F32)] * 2
         + [pltpu.VMEM((64, GRID), F32)]
-        + [message_z] * 2
-        + [message_y] * 4
-        + [message_z] * 2
-        + [pltpu.VMEM((256, 128), F32)] * 2
-        + [pltpu.VMEM((320, GRID), F32)]
+        + [tall] * 2
+        + [short] * 2
+        + [both] * 4
+        + [short] * 2
+        + [tall] * 2
+        + [short] * 3
         + [pltpu.VMEM((ROWS, GRID), BF16)] * 2
         + [
             pltpu.VMEM((3, ATOMS_DEV), F32),
@@ -681,9 +775,12 @@
             pltpu.VMEM((1, ATOMS_DEV), F32),
             pltpu.VMEM((3, ATOMS_DEV), F32),
             pltpu.VMEM((3, ATOMS_DEV), jnp.int32),
+            pltpu.VMEM((32, 128), F32),
+            pltpu.VMEM((48, 128), F32),
             pltpu.SemaphoreType.DMA((8,)),
-            pltpu.SemaphoreType.DMA((4, NPEER)),
-            pltpu.SemaphoreType.DMA((4, NPEER)),
+            pltpu.SemaphoreType.DMA((4,)),
+            pltpu.SemaphoreType.DMA((8,)),
+            pltpu.SemaphoreType.DMA((8,)),
         ],
         compiler_params=pltpu.CompilerParams(collective_id=0, has_side_effects=True),
         name="forces",

time: 84.2 us -> 79.8 us (0.948)
  Pallas kernels: 81.8 us -> 77.4 us
    pallas_call x1, Pallas kernels: 81.8 us -> 77.4 us  [solve(): pl.pallas_call(solve_kernel, out_shape=jax.ShapeDtypeStruct((3, ATOMS_DEV...]
where the time goes in v2:
time: 79.8 us; the launch traced here: 79.7 us
  Pallas kernels  77.4 us (97%)
  local copies, waits for them, and re-layouts  1.64 us (2%)
    pallas_call x1, Pallas kernels, solve(): pl.pallas_call(solve_kernel, out_shape=jax.ShapeDtypeStruct((3, ATOMS_DEV...  77.4 us
    unnamed x1, local copies, waits for them, and re-layouts  1.64 us

profile of v2, /device:TPU:1, one launch (start us, length us, event | category | flops | bytes accessed | tf_op | source)
XLA Modules:
  0.0 79.7 jit_solution(11635882937092200092)
XLA Ops:
  0.7 77.4 %forces.1 = f32[3,12288]{1,0:T(4,128)} custom-call(s32[1,16]{1,0:T(1,128)} %live_ref.1, s32[1,16]{1,0:T(1,128)} %send_ref.1, f32[1]{0:T(128)S(6)} %copy.14.screening_ref, f32[1,12288]{1,0:T(1,128)} %bitcast.1, f32[3,12288]{1,0:T(4,128)} %frac_ref.1, s32[3,12288]{1,0:T(4,128)} %cell_ref.1, f32[3,256]{1,0:T(4,128)} %moduli_ref.1, ...), custom_call_target="tpu_custom_call" | custom-call | tf_op jit(solution)/shard_map/forces/pallas_call | solution.py:754
  78.0 1.6 %copy.15 = f32[3,12288]{1,0:T(4,128)} copy(f32[3,12288]{1,0:T(4,128)} %forces.1) | data formatting | bytes 294912

commit v3 on v2

--- a/solution.py
+++ b/solution.py
@@ -16,9 +16,10 @@
 NPEER = 16
 CHUNK = 512
 SPREAD_UNROLL = 4
-GATHER_UNROLL = 6
+GATHER_UNROLL = 4
+EARLY = 8
+CORE = 256
 ROWS = 384
-SLOT_Z = 24
 MESH = pl.DeviceIdType.MESH
 BF16 = jnp.bfloat16
 F32 = jnp.float32
@@ -69,11 +70,7 @@
 
 def tables_z():
     local, block = np.meshgrid(np.arange(16), np.arange(16), indexing="ij")
-    wave = kz_of(block, local).reshape(-1)
-    place = np.arange(SLOT_Z)
-    places = (16 * np.arange(16)[:, None] + place[None, :]).reshape(-1)
-    pad = np.tile(place >= 19, 16)[None, :]
-    parts = [np.where(pad, 0.0, part) for part in cos_sin(wave, places)]
+    parts = cos_sin(kz_of(block, local).reshape(-1), np.arange(256))
     return np.concatenate(parts, 0), np.concatenate([part.T for part in parts], 0)
 
 
@@ -213,7 +210,11 @@
     lax.fori_loop(0, ATOMS_DEV // (n * SPREAD_UNROLL), step, 0)
 
 
-def gather_atoms(charge_ref, frac_ref, cell_ref, out_ref, p_hi, p_lo, when_lent_done):
+def gather_atoms(
+    chunks, own, rim, charge_ref, frac_ref, cell_ref, out_ref, p_hi, p_lo, after_first=None
+):
+    base = 0 if own else CORE
+    rows = slice(base, ROWS if rim else CORE)
     n = 256
 
     def piece_of(first):
@@ -231,7 +232,7 @@
                 )
             )
         w_hi, w_lo, s_hi, s_lo = (jnp.concatenate(part, 1) for part in zip(*columns))
-        hi, lo = p_hi[...], p_lo[...]
+        hi, lo = p_hi[rows, :], p_lo[rows, :]
         along_all = nn_dot(hi, w_hi) + nn_dot(hi, w_lo) + nn_dot(lo, w_hi)
         steep_all = nn_dot(hi, s_hi) + nn_dot(hi, s_lo) + nn_dot(lo, s_hi)
         results = []
@@ -246,15 +247,15 @@
             yw_main, yw_halo = narrow_tables(cells, weights, 1)
             ys_main, ys_halo = narrow_tables(cells, slopes, 1)
             sums = [jnp.zeros((16, 128), F32)] * 3
-            for y in range(19):
-                row = 16 * y if y < 16 else 320 + 16 * (y - 16)
+            for y in range(0 if own else 16, 19 if rim else 16):
+                row = 16 * y if y < 16 else 320 + 16 * (y - 16) - base
                 yw = wide(yw_main[y : y + 1] if y < 16 else yw_halo[y - 16 : y - 15], 16)
                 ys = wide(ys_main[y : y + 1] if y < 16 else ys_halo[y - 16 : y - 15], 16)
                 piece, slope = along[row : row + 16], steep[row : row + 16]
                 sums = [sums[0] + yw * piece, sums[1] + ys * piece, sums[2] + yw * slope]
             rims = [jnp.zeros((8, 128), F32)] * 3
-            for pair in range(10):
-                row = 256 + 8 * pair if pair < 8 else 368 + 8 * (pair - 8)
+            for pair in range(10 if rim else 0):
+                row = (256 + 8 * pair if pair < 8 else 368 + 8 * (pair - 8)) - base
                 yw = pair_pattern(yw_main, pair) if pair < 8 else pair_pattern(yw_halo, pair - 8)
                 ys = pair_pattern(ys_main, pair) if pair < 8 else pair_pattern(ys_halo, pair - 8)
                 piece, slope = along[row : row + 8], steep[row : row + 8]
@@ -271,17 +272,22 @@
                 )
             )
         q = charge_ref[:, pl.ds(first, n)]
-        out_ref[:, pl.ds(first, n)] = jnp.concatenate(results, 1) * -q
-
+        result = jnp.concatenate(results, 1) * -q
+        if not own:
+            result = result + out_ref[:, pl.ds(first, n)]
+        out_ref[:, pl.ds(first, n)] = result
+
+    low, high = chunks
     per_step = GATHER_UNROLL * CHUNK
 
     def step(i, carry):
         for u in range(per_step // n):
-            piece_of(pl.multiple_of(i * per_step + u * n, n))
-        pl.when(i == SEND_MAX * BLOCK // per_step)(when_lent_done)
+            piece_of(pl.multiple_of(low * CHUNK + i * per_step + u * n, n))
+        if after_first is not None:
+            pl.when(i == 0)(after_first)
         return carry
 
-    lax.fori_loop(0, ATOMS_DEV // per_step, step, 0)
+    lax.fori_loop(0, (high - low) // GATHER_UNROLL, step, 0)
 
 
 def turn(arrays):
@@ -435,18 +441,15 @@
     tile_ref,
     pot_ref,
     rim_in,
-    send_10,
-    recv_10,
-    send_11,
-    recv_11,
+    planes_out,
+    send_1,
+    recv_1,
     send_2,
     recv_2,
     send_3,
     recv_3,
-    send_40,
-    recv_40,
-    send_41,
-    recv_41,
+    send_4,
+    recv_4,
     straight_0,
     straight_1,
     crossed_0,
@@ -487,7 +490,10 @@
     for load in loads:
         load.start()
 
-    before = (b + 15) % 16
+    before, after = (b + 15) % 16, (b + 1) % 16
+    before_z, after_z = (a + 15) % 16, (a + 1) % 16
+    for peer in ((before_z, before), (after_z, after)):
+        pl.semaphore_signal(barrier, inc=1, device_id=peer, device_id_type=MESH)
     live = live_ref[0, b]
     kept = live - send_ref[0, b]
     kept_before = live_ref[0, before] - send_ref[0, before]
@@ -495,7 +501,7 @@
     spread_atoms(live * BLOCK, charge_ref, frac_ref, cell_ref, tile_ref)
     for load in loads:
         load.wait()
-    pl.semaphore_wait(barrier, 2 * (NPEER - 1))
+    pl.semaphore_wait(barrier, 2 * NPEER)
 
     leaving = []
 
@@ -562,48 +568,56 @@
             return every.wait_recv, forward
         return every.wait_recv
 
-    rim = pltpu.make_async_remote_copy(
-        src_ref=tile_ref.at[pl.ds(320, 64), :],
-        dst_ref=rim_in,
-        send_sem=rim_sems.at[0],
-        recv_sem=rim_sems.at[1],
-        device_id=(a, (b + 1) % 16),
-        device_id_type=MESH,
-    )
-    rim.start()
+    def rim_copy(index, source, target, peer):
+        return pltpu.make_async_remote_copy(
+            src_ref=source,
+            dst_ref=target,
+            send_sem=rim_sems.at[2 * index],
+            recv_sem=rim_sems.at[2 * index + 1],
+            device_id=peer,
+            device_id_type=MESH,
+        )
+
+    rims = [
+        rim_copy(k, tile_ref.at[pl.ds(first, size), :], rim_in.at[pl.ds(first - 256, size), :], peer)
+        for k, (first, size, peer) in enumerate(
+            ((368, 16, (after_z, after)), (256, 64, (after_z, b)), (320, 48, (a, after)))
+        )
+    ]
+    for copy in rims:
+        copy.start()
 
     def transform_x(value):
         high, low = split(value)
         return nn_dot(high, fx[0]) + nn_dot(high, fx[1]) + nn_dot(low, fx[0])
 
-    spectrum = transform_x(tile_ref[0:320, :])
-    rim.wait()
+    spectrum = transform_x(tile_ref[0:256, :])
+    for copy in rims:
+        copy.wait()
     extra = transform_x(rim_in[...])
-    spectrum = jnp.concatenate(
-        [
-            spectrum[0:48] + extra[0:48],
-            spectrum[48:256],
-            spectrum[256:272] + extra[48:64],
-            spectrum[272:320],
-        ],
-        0,
-    )
-    iota = lax.broadcasted_iota(jnp.int32, (8, 128), 0)
-    pieces = []
+    iota = lax.broadcasted_iota(jnp.int32, (8, 256), 0)
+    planes = [spectrum[16 * y : 16 * y + 16] for y in range(16)]
     for y in range(16):
-        row = 256 + 8 * (y // 2)
-        first, second = spectrum[row : row + 8, :128], spectrum[row : row + 8, 128:]
-        if y % 2 == 0:
-            halo = jnp.where(iota < 4, first, pltpu.roll(second, 4, 0))
-        else:
-            halo = jnp.where(iota < 4, pltpu.roll(first, 4, 0), second)
-        pieces.append(jnp.concatenate([spectrum[16 * y : 16 * y + 16, :128], halo], 0))
-    for peer, piece in enumerate(turn(pieces)):
-        send_10[24 * peer : 24 * peer + 24, :] = piece
-    arrive_10 = exchange(0, send_10, recv_10, 24, True)
-    for peer, piece in enumerate(turn([spectrum[16 * y : 16 * y + 16, 128:] for y in range(16)])):
-        send_11[16 * peer : 16 * peer + 16, :] = piece
-    arrive_11, forward = exchange(1, send_11, recv_11, 16, True, (held_1, 0))
+        halo = extra[8 * (y // 2) : 8 * (y // 2) + 8]
+        if y < 4:
+            halo = halo + extra[112 + 8 * (y // 2) : 120 + 8 * (y // 2)]
+        halo = jnp.where(iota < 4, halo if y % 2 == 0 else pltpu.roll(halo, 4, 0), 0.0)
+        plane = jnp.concatenate([planes[y][:8] + halo, planes[y][8:]], 0)
+        planes[y] = plane + extra[64 + 16 * y : 80 + 16 * y] if y < 3 else plane
+
+    def send_lines(stream):
+        lanes = slice(128 * stream, 128 * stream + 128)
+        for peer, piece in enumerate(turn([plane[:, lanes] for plane in planes])):
+            first = 256 * stream + 16 * peer
+            send_1[first : first + 16, :] = piece
+
+    def part(ref, stream):
+        return ref.at[pl.ds(256 * stream, 256), :]
+
+    send_lines(0)
+    arrive_10 = exchange(0, part(send_1, 0), part(recv_1, 0), 16, True)
+    send_lines(1)
+    arrive_11, forward = exchange(1, part(send_1, 1), part(recv_1, 1), 16, True, (held_1, 0))
     tables_of_influence(
         moduli_ref, screening_ref[0], a, b, (straight_0, straight_1, crossed_0)
     )
@@ -623,22 +637,12 @@
         return both[:rows] + wide(sign, rows) * pltpu.roll(both[rows:], 64, 1)
 
     def stage_z(stream):
-        if stream == 0:
-            lines = recv_10[...]
-        else:
-            lines = []
-            for k in range(16):
-                lines += [
-                    recv_11[16 * k : 16 * k + 16, :],
-                    pltpu.roll(recv_10[24 * k + 16 : 24 * k + 24, :], 4, 0),
-                ]
-            lines = jnp.concatenate(lines, 0)
+        lines = recv_1[256 * stream : 256 * stream + 256, :]
         waves = joined(product(fz, lines), forward_sign)
         turned = turn([waves[16 * k : 16 * k + 16] for k in range(16)])
         for y in range(16):
             send_2[pl.ds(256 * stream + y, 16, stride=16), :] = turned[y]
-        rows = pl.ds(256 * stream, 256)
-        return exchange(2 + stream, send_2.at[rows, :], recv_2.at[rows, :], 16, False)
+        return exchange(2 + stream, part(send_2, stream), part(recv_2, stream), 16, False)
 
     def stage_y(stream):
         lines = recv_2[256 * stream : 256 * stream + 256, :]
@@ -653,14 +657,17 @@
             waves = waves + joined(both[:, 128:], forward_sign) * crossed_0[...]
         else:
             waves = joined(product(fy, lines), forward_sign) * straight_1[...]
-        rows = pl.ds(256 * stream, 256)
-        send_3[rows, :] = joined(product(fy, waves), -forward_sign)
-        return exchange(4 + stream, send_3.at[rows, :], recv_3.at[rows, :], 16, False)
+        first = 256 * stream
+        send_3[first : first + 256, :] = joined(product(fy, waves), -forward_sign)
+        return exchange(4 + stream, part(send_3, stream), part(recv_3, stream), 16, False)
 
     def stage_z_back(stream):
         pieces = [recv_3[pl.ds(256 * stream + y, 16, stride=16), :] for y in range(16)]
         lines = jnp.concatenate(turn(pieces), 0)
-        return joined(product(gz, lines), -forward_sign)
+        first = 256 * stream
+        send_4[first : first + 256, :] = joined(product(gz, lines), -forward_sign)
+        relay = (held_4, 2) if stream else None
+        return exchange(6 + stream, part(send_4, stream), part(recv_4, stream), 16, True, relay)
 
     arrive_10()
     arrive_20 = stage_z(0)
@@ -671,76 +678,63 @@
     arrive_21()
     arrive_31 = stage_y(1)
     arrive_30()
-    back = stage_z_back(0)
-    for k in range(16):
-        send_40[16 * k : 16 * k + 16, :] = back[24 * k : 24 * k + 16]
-        send_41[24 * k + 16 : 24 * k + 24, :] = back[24 * k + 16 : 24 * k + 24]
-    arrive_40 = exchange(6, send_40, recv_40, 16, True)
+    arrive_40 = stage_z_back(0)
     arrive_31()
-    back = stage_z_back(1)
-    for k in range(16):
-        send_41[24 * k : 24 * k + 16, :] = back[24 * k : 24 * k + 16]
-        send_41[24 * k + 16 : 24 * k + 24, :] += pltpu.roll(back[24 * k + 16 : 24 * k + 24], 4, 0)
-    arrive_41, forward = exchange(7, send_41, recv_41, 24, True, (held_4, 2))
+    arrive_41, forward = stage_z_back(1)
     handed_first(
         live, kept, charge_ref, frac_ref, cell_ref, charge_in_order, frac_in_order, cell_in_order
     )
     forward()
+    def lines_back(stream):
+        return turn(
+            [recv_4[256 * stream + 16 * k : 256 * stream + 16 * k + 16, :] for k in range(16)]
+        )
+
     arrive_40()
-    turned_0 = turn([recv_40[16 * k : 16 * k + 16, :] for k in range(16)])
+    turned_0 = lines_back(0)
     arrive_41()
-    turned_1 = turn([recv_41[24 * k : 24 * k + 24, :] for k in range(16)])
-
-    lines = [jnp.concatenate([first, second[:16]], 1) for first, second in zip(turned_0, turned_1)]
-    rims = []
+    turned_1 = lines_back(1)
+
+    high, low = split(
+        jnp.concatenate([jnp.concatenate(pair, 1) for pair in zip(turned_0, turned_1)], 0)
+    )
+    value = nn_dot(high, gx[0]) + nn_dot(high, gx[1]) + nn_dot(low, gx[0])
+    pot_ref[0:256, :] = value
     for pair in range(8):
-        even, odd = turned_1[2 * pair][16:24], turned_1[2 * pair + 1][16:24]
-        first = jnp.where(iota < 4, even, pltpu.roll(odd, 4, 0))
-        second = jnp.where(iota < 4, pltpu.roll(even, 4, 0), odd)
-        rims.append(jnp.concatenate([first, second], 1))
-
-    def back_x(value):
-        high, low = split(value)
-        return nn_dot(high, gx[0]) + nn_dot(high, gx[1]) + nn_dot(low, gx[0])
-
-    value = back_x(jnp.concatenate(lines[:3] + rims[:2], 0))
-    pot_ref[0:48, :] = value[0:48]
-    pot_ref[256:272, :] = value[48:64]
+        even, odd = value[32 * pair : 32 * pair + 8], value[32 * pair + 16 : 32 * pair + 24]
+        planes_out[8 * pair : 8 * pair + 8, :] = jnp.where(iota < 4, even, pltpu.roll(odd, 4, 0))
     copies = [
-        pltpu.make_async_remote_copy(
-            src_ref=pot_ref.at[pl.ds(source, size), :],
-            dst_ref=pot_ref.at[pl.ds(target, size), :],
-            send_sem=rim_sems.at[2 + 2 * k],
-            recv_sem=rim_sems.at[3 + 2 * k],
-            device_id=(a, before),
-            device_id_type=MESH,
+        rim_copy(3 + k, source.at[pl.ds(0, size), :], pot_ref.at[pl.ds(target, size), :], peer)
+        for k, (source, target, size, peer) in enumerate(
+            (
+                (planes_out, 368, 16, (before_z, before)),
+                (planes_out, 256, 64, (before_z, b)),
+                (pot_ref, 320, 48, (a, before)),
+            )
         )
-        for k, (source, target, size) in enumerate(((0, 320, 48), (256, 368, 16)))
     ]
     for copy in copies:
         copy.start()
-    value = back_x(jnp.concatenate(lines[3:] + rims[2:], 0))
-    pot_ref[48:256, :] = value[:208]
-    pot_ref[272:320, :] = value[208:]
     for leave in leaving:
         leave()
+
+    def keep_parts(rows):
+        high, low = split(pot_ref[rows, :])
+        p_hi[rows, :] = high
+        p_lo[rows, :] = low
+
+    def compute(*split_of, after_first=None):
+        atoms = (charge_in_order, frac_in_order, cell_in_order)
+        gather_atoms(*split_of, *atoms, forces, p_hi, p_lo, after_first)
+
+    hand_on = rim_copy(6, forces.at[:, pl.ds(0, SEND_MAX * BLOCK)], guests, (a, after))
+    keep_parts(slice(0, CORE))
+    compute((0, EARLY), True, False)
     for copy in copies:
         copy.wait()
-    high, low = split(pot_ref[...])
-    p_hi[...] = high
-    p_lo[...] = low
-
-    hand_on = pltpu.make_async_remote_copy(
-        src_ref=forces.at[:, pl.ds(0, SEND_MAX * BLOCK)],
-        dst_ref=guests,
-        send_sem=rim_sems.at[6],
-        recv_sem=rim_sems.at[7],
-        device_id=(a, (b + 1) % 16),
-        device_id_type=MESH,
-    )
-    gather_atoms(
-        charge_in_order, frac_in_order, cell_in_order, forces, p_hi, p_lo, hand_on.start
-    )
+    keep_parts(slice(CORE, ROWS))
+    compute((0, EARLY), False, True)
+    compute((EARLY, ATOMS_DEV // CHUNK), True, True, after_first=hand_on.start)
     hand_on.wait()
     place_forces(kept, kept_before, arriving, forces, guests, out_ref)
 
@@ -749,8 +743,7 @@
     tables = []
     for table in (forward_x(), inverse_x(), *tables_z(), table_y()):
         tables.append(jnp.asarray(np.stack(split_np(table))))
-    short, tall = pltpu.VMEM((256, 128), F32), pltpu.VMEM((384, 128), F32)
-    both = pltpu.VMEM((512, 128), F32)
+    short, both = pltpu.VMEM((256, 128), F32), pltpu.VMEM((512, 128), F32)
     return pl.pallas_call(
         solve_kernel,
         out_shape=jax.ShapeDtypeStruct((3, ATOMS_DEV), F32),
@@ -761,12 +754,8 @@
         scratch_shapes=[pltpu.VMEM(table.shape, BF16) for table in tables]
         + [pltpu.SemaphoreType.DMA((len(tables),))]
         + [pltpu.VMEM((ROWS, GRID), F32)] * 2
-        + [pltpu.VMEM((64, GRID), F32)]
-        + [tall] * 2
-        + [short] * 2
-        + [both] * 4
-        + [short] * 2
-        + [tall] * 2
+        + [pltpu.VMEM((128, GRID), F32), pltpu.VMEM((64, GRID), F32)]
+        + [both] * 8
         + [short] * 3
         + [pltpu.VMEM((ROWS, GRID), BF16)] * 2
         + [
@@ -776,8 +765,8 @@
             pltpu.VMEM((3, ATOMS_DEV), F32),
             pltpu.VMEM((3, ATOMS_DEV), jnp.int32),
             pltpu.VMEM((32, 128), F32),
-            pltpu.VMEM((48, 128), F32),
-            pltpu.SemaphoreType.DMA((8,)),
+            pltpu.VMEM((32, 128), F32),
+            pltpu.SemaphoreType.DMA((14,)),
             pltpu.SemaphoreType.DMA((4,)),
             pltpu.SemaphoreType.DMA((8,)),
             pltpu.SemaphoreType.DMA((8,)),

time: 79.8 us -> 78.3 us (0.981)
  Pallas kernels: 77.4 us -> 75.9 us
    pallas_call x1, Pallas kernels: 77.4 us -> 75.9 us  [solve(): pl.pallas_call(solve_kernel, out_shape=jax.ShapeDtypeStruct((3, ATOMS_DEV...]
where the time goes in v3:
time: 78.3 us; the launch traced here: 78.2 us
  Pallas kernels  75.9 us (97%)
  local copies, waits for them, and re-layouts  1.64 us (2%)
    pallas_call x1, Pallas kernels, solve(): pl.pallas_call(solve_kernel, out_shape=jax.ShapeDtypeStruct((3, ATOMS_DEV...  75.9 us
    unnamed x1, local copies, waits for them, and re-layouts  1.64 us

profile of v3, /device:TPU:1, one launch (start us, length us, event | category | flops | bytes accessed | tf_op | source)
XLA Modules:
  0.0 78.2 jit_solution(1848215417828320558)
XLA Ops:
  0.7 75.9 %forces.1 = f32[3,12288]{1,0:T(4,128)} custom-call(s32[1,16]{1,0:T(1,128)} %live_ref.1, s32[1,16]{1,0:T(1,128)} %send_ref.1, f32[1]{0:T(128)S(6)} %copy.14.screening_ref, f32[1,12288]{1,0:T(1,128)} %bitcast.1, f32[3,12288]{1,0:T(4,128)} %frac_ref.1, s32[3,12288]{1,0:T(4,128)} %cell_ref.1, f32[3,256]{1,0:T(4,128)} %moduli_ref.1, ...), custom_call_target="tpu_custom_call" | custom-call | tf_op jit(solution)/shard_map/forces/pallas_call | solution.py:747
  76.6 1.6 %copy.15 = f32[3,12288]{1,0:T(4,128)} copy(f32[3,12288]{1,0:T(4,128)} %forces.1) | data formatting | bytes 294912

commit v4 on v3

--- a/solution.py
+++ b/solution.py
@@ -210,28 +210,48 @@
     lax.fori_loop(0, ATOMS_DEV // (n * SPREAD_UNROLL), step, 0)
 
 
+def wide_x_tables(cells, weights, slopes):
+    columns = []
+    for group in range(cells.shape[1] // 128):
+        lanes = slice(128 * group, 128 * group + 128)
+        columns.append(
+            x_tables(
+                cells[:, lanes],
+                high_low([w[2:3, lanes] for w in weights])
+                + high_low([w[2:3, lanes] for w in slopes]),
+            )
+        )
+    return [jnp.concatenate(part, 1) for part in zip(*columns)]
+
+
+def hold_x_tables(frac_ref, cell_ref, held):
+    def step(index, carry):
+        place = pl.ds(pl.multiple_of(index * 256, 256), 256)
+        t = frac_ref[:, place]
+        tables = wide_x_tables(cell_ref[:, place], spline_weights(t), spline_slopes(t))
+        for k, table in enumerate(tables):
+            held[k, index] = table
+        return carry
+
+    lax.fori_loop(0, EARLY * CHUNK // 256, step, 0)
+
+
 def gather_atoms(
-    chunks, own, rim, charge_ref, frac_ref, cell_ref, out_ref, p_hi, p_lo, after_first=None
+    chunks, own, rim, charge_ref, frac_ref, cell_ref, out_ref, p_hi, p_lo, held=None, after_first=None
 ):
     base = 0 if own else CORE
     rows = slice(base, ROWS if rim else CORE)
     n = 256
 
-    def piece_of(first):
+    def piece_of(index):
+        first = pl.multiple_of(index * n, n)
         t = frac_ref[:, pl.ds(first, n)]
         cells_all = cell_ref[:, pl.ds(first, n)]
         weights_all, slopes_all = spline_weights(t), spline_slopes(t)
-        columns = []
-        for group in range(n // 128):
-            lanes = slice(128 * group, 128 * group + 128)
-            columns.append(
-                x_tables(
-                    cells_all[:, lanes],
-                    high_low([w[2:3, lanes] for w in weights_all])
-                    + high_low([w[2:3, lanes] for w in slopes_all]),
-                )
-            )
-        w_hi, w_lo, s_hi, s_lo = (jnp.concatenate(part, 1) for part in zip(*columns))
+        if held is None:
+            w_hi, w_lo, s_hi, s_lo = wide_x_tables(cells_all, weights_all, slopes_all)
+        else:
+            w_hi, w_lo, s_hi, s_lo = (held[k, index] for k in range(4))
         hi, lo = p_hi[rows, :], p_lo[rows, :]
         along_all = nn_dot(hi, w_hi) + nn_dot(hi, w_lo) + nn_dot(lo, w_hi)
         steep_all = nn_dot(hi, s_hi) + nn_dot(hi, s_lo) + nn_dot(lo, s_hi)
@@ -282,7 +302,7 @@
 
     def step(i, carry):
         for u in range(per_step // n):
-            piece_of(pl.multiple_of(low * CHUNK + i * per_step + u * n, n))
+            piece_of(low * (CHUNK // n) + i * (per_step // n) + u)
         if after_first is not None:
             pl.when(i == 0)(after_first)
         return carry
@@ -460,6 +480,7 @@
     charge_in_order,
     frac_in_order,
     cell_in_order,
+    held,
     held_1,
     held_4,
     rim_sems,
@@ -530,13 +551,13 @@
             step = (a // 2 + 6) % 8 * 2
             origin = (a // 2 + 2) % 8 * 2 + a % 2
             for k in range(2):
-                held = buffer.at[pl.ds(k * size, size), :]
+                leg = buffer.at[pl.ds(k * size, size), :]
                 copy(
-                    src.at[rows_of(peers[k]), :], held, step + a % 2, send_sem, relay_sems.at[sems]
+                    src.at[rows_of(peers[k]), :], leg, step + a % 2, send_sem, relay_sems.at[sems]
                 ).start()
                 passing.append(
                     copy(
-                        held,
+                        leg,
                         dst.at[rows_of(origin), :],
                         step + (a + 1 - k) % 2,
                         relay_sems.at[sems + 1],
@@ -551,17 +572,17 @@
         leaving.append(every.wait_send)
         if relay is not None:
             both = pl.ds(0, 2 * size)
-            held = copy(
+            legs = copy(
                 buffer.at[both, :],
                 buffer.at[both, :],
                 peers[0],
                 relay_sems.at[sems + 1],
                 relay_sems.at[sems],
             )
-            leaving.append(held.wait_send)
+            leaving.append(legs.wait_send)
 
             def forward():
-                held.wait_recv()
+                legs.wait_recv()
                 for message in passing:
                     message.start()
 
@@ -592,6 +613,10 @@
         return nn_dot(high, fx[0]) + nn_dot(high, fx[1]) + nn_dot(low, fx[0])
 
     spectrum = transform_x(tile_ref[0:256, :])
+    handed_first(
+        live, kept, charge_ref, frac_ref, cell_ref, charge_in_order, frac_in_order, cell_in_order
+    )
+    hold_x_tables(frac_in_order, cell_in_order, held)
     for copy in rims:
         copy.wait()
     extra = transform_x(rim_in[...])
@@ -681,9 +706,6 @@
     arrive_40 = stage_z_back(0)
     arrive_31()
     arrive_41, forward = stage_z_back(1)
-    handed_first(
-        live, kept, charge_ref, frac_ref, cell_ref, charge_in_order, frac_in_order, cell_in_order
-    )
     forward()
     def lines_back(stream):
         return turn(
@@ -723,17 +745,17 @@
         p_hi[rows, :] = high
         p_lo[rows, :] = low
 
-    def compute(*split_of, after_first=None):
+    def compute(*split_of, **options):
         atoms = (charge_in_order, frac_in_order, cell_in_order)
-        gather_atoms(*split_of, *atoms, forces, p_hi, p_lo, after_first)
+        gather_atoms(*split_of, *atoms, forces, p_hi, p_lo, **options)
 
     hand_on = rim_copy(6, forces.at[:, pl.ds(0, SEND_MAX * BLOCK)], guests, (a, after))
     keep_parts(slice(0, CORE))
-    compute((0, EARLY), True, False)
+    compute((0, EARLY), True, False, held=held)
     for copy in copies:
         copy.wait()
     keep_parts(slice(CORE, ROWS))
-    compute((0, EARLY), False, True)
+    compute((0, EARLY), False, True, held=held)
     compute((EARLY, ATOMS_DEV // CHUNK), True, True, after_first=hand_on.start)
     hand_on.wait()
     place_forces(kept, kept_before, arriving, forces, guests, out_ref)
@@ -764,6 +786,7 @@
             pltpu.VMEM((1, ATOMS_DEV), F32),
             pltpu.VMEM((3, ATOMS_DEV), F32),
             pltpu.VMEM((3, ATOMS_DEV), jnp.int32),
+            pltpu.VMEM((4, EARLY * CHUNK // 256, 256, 256), BF16),
             pltpu.VMEM((32, 128), F32),
             pltpu.VMEM((32, 128), F32),
             pltpu.SemaphoreType.DMA((14,)),

time: 78.3 us -> 76.3 us (0.974)
  Pallas kernels: 75.9 us -> 73.9 us
    pallas_call x1, Pallas kernels: 75.9 us -> 73.9 us  [solve(): pl.pallas_call(solve_kernel, out_shape=jax.ShapeDtypeStruct((3, ATOMS_DEV...]
where the time goes in v4:
time: 76.3 us; the launch traced here: 76.2 us
  Pallas kernels  73.9 us (97%)
  local copies, waits for them, and re-layouts  1.64 us (2%)
    pallas_call x1, Pallas kernels, solve(): pl.pallas_call(solve_kernel, out_shape=jax.ShapeDtypeStruct((3, ATOMS_DEV...  73.9 us
    unnamed x1, local copies, waits for them, and re-layouts  1.64 us

profile of v4, /device:TPU:1, one launch (start us, length us, event | category | flops | bytes accessed | tf_op | source)
XLA Modules:
  0.0 76.2 jit_solution(12348844469771012488)
XLA Ops:
  0.7 73.9 %forces.1 = f32[3,12288]{1,0:T(4,128)} custom-call(s32[1,16]{1,0:T(1,128)} %live_ref.1, s32[1,16]{1,0:T(1,128)} %send_ref.1, f32[1]{0:T(128)S(6)} %copy.14.screening_ref, f32[1,12288]{1,0:T(1,128)} %bitcast.1, f32[3,12288]{1,0:T(4,128)} %frac_ref.1, s32[3,12288]{1,0:T(4,128)} %cell_ref.1, f32[3,256]{1,0:T(4,128)} %moduli_ref.1, ...), custom_call_target="tpu_custom_call" | custom-call | tf_op jit(solution)/shard_map/forces/pallas_call | solution.py:769
  74.6 1.6 %copy.15 = f32[3,12288]{1,0:T(4,128)} copy(f32[3,12288]{1,0:T(4,128)} %forces.1) | data formatting | bytes 294912

commit v5 on v4

--- a/solution.py
+++ b/solution.py
@@ -17,7 +17,7 @@
 CHUNK = 512
 SPREAD_UNROLL = 4
 GATHER_UNROLL = 4
-EARLY = 8
+EARLY = 12
 CORE = 256
 ROWS = 384
 MESH = pl.DeviceIdType.MESH
@@ -224,7 +224,7 @@
     return [jnp.concatenate(part, 1) for part in zip(*columns)]
 
 
-def hold_x_tables(frac_ref, cell_ref, held):
+def hold_x_tables(pieces, frac_ref, cell_ref, held):
     def step(index, carry):
         place = pl.ds(pl.multiple_of(index * 256, 256), 256)
         t = frac_ref[:, place]
@@ -233,7 +233,7 @@
             held[k, index] = table
         return carry
 
-    lax.fori_loop(0, EARLY * CHUNK // 256, step, 0)
+    lax.fori_loop(*pieces, step, 0)
 
 
 def gather_atoms(
@@ -616,7 +616,7 @@
     handed_first(
         live, kept, charge_ref, frac_ref, cell_ref, charge_in_order, frac_in_order, cell_in_order
     )
-    hold_x_tables(frac_in_order, cell_in_order, held)
+    hold_x_tables((0, 16), frac_in_order, cell_in_order, held)
     for copy in rims:
         copy.wait()
     extra = transform_x(rim_in[...])
@@ -646,6 +646,7 @@
     tables_of_influence(
         moduli_ref, screening_ref[0], a, b, (straight_0, straight_1, crossed_0)
     )
+    hold_x_tables((16, EARLY * CHUNK // 256), frac_in_order, cell_in_order, held)
     forward()
 
     half = lax.broadcasted_iota(jnp.int32, (1, 128), 1) < 64

time: 76.3 us -> 74.5 us (0.976)
  Pallas kernels: 73.9 us -> 72 us
    pallas_call x1, Pallas kernels: 73.9 us -> 72 us  [solve(): pl.pallas_call(solve_kernel, out_shape=jax.ShapeDtypeStruct((3, ATOMS_DEV...]
where the time goes in v5:
time: 74.5 us; the launch traced here: 74.3 us
  Pallas kernels  72 us (97%)
  local copies, waits for them, and re-layouts  1.64 us (2%)
    pallas_call x1, Pallas kernels, solve(): pl.pallas_call(solve_kernel, out_shape=jax.ShapeDtypeStruct((3, ATOMS_DEV...  72 us
    unnamed x1, local copies, waits for them, and re-layouts  1.64 us

profile of v5, /device:TPU:1, one launch (start us, length us, event | category | flops | bytes accessed | tf_op | source)
XLA Modules:
  0.0 74.3 jit_solution(17102350761068695565)
XLA Ops:
  0.7 72.0 %forces.1 = f32[3,12288]{1,0:T(4,128)} custom-call(s32[1,16]{1,0:T(1,128)} %live_ref.1, s32[1,16]{1,0:T(1,128)} %send_ref.1, f32[1]{0:T(128)S(6)} %copy.14.screening_ref, f32[1,12288]{1,0:T(1,128)} %bitcast.1, f32[3,12288]{1,0:T(4,128)} %frac_ref.1, s32[3,12288]{1,0:T(4,128)} %cell_ref.1, f32[3,256]{1,0:T(4,128)} %moduli_ref.1, ...), custom_call_target="tpu_custom_call" | custom-call | tf_op jit(solution)/shard_map/forces/pallas_call | solution.py:770
  72.7 1.6 %copy.15 = f32[3,12288]{1,0:T(4,128)} copy(f32[3,12288]{1,0:T(4,128)} %forces.1) | data formatting | bytes 294912
